TPU v7x, 768 devices: a whole 4x8x12 slice. The times are simulated.
768 devices in a mesh: grp: 8 (over y_hi, core), row: 24 (over y_lo, z), col: 4 (over x).
Axes of the slice: x: 4, y: 8 (y_hi: 4, y_lo: 2; y = y_hi * 2 + y_lo), z: 12, core: 2. Of those that a mesh axis runs over, the one named last changes fastest.
Arguments:
- field: float32 [8, 8, 3072, 1536], P(None, 'grp', 'row', 'col'), may hold values from -6 to 6
- previous: bfloat16 [8, 8, 3072, 1536], P(None, 'grp', 'row', 'col'), may hold values from -6 to 6
- kappa: float32 [8, 3072, 1536], P('grp', 'row', 'col'), may hold values from 0.02 to 0.1
- rates: float32 [8], replicated, may hold values from 0.5 to 1.6
- speeds: float32 [8, 3], replicated, may hold values from -0.5 to 0.5
- basis_x: bfloat16 [3072, 128], replicated, may hold values from -0.109375 to 0.109375
- basis_y: bfloat16 [1536, 128], replicated, may hold values from -0.15625 to 0.15625
Outputs:
- advanced: float32 [8, 8, 3072, 1536], P(None, 'grp', 'row', 'col')
- core: float32 [8, 8, 128, 128], P(None, 'grp')
- gram_x: float32 [3072, 128], P('row')
- gram_y: float32 [1536, 128], P(('col', 'row'))
All inputs are finite; a program needn't handle non-finite values.
Results may differ from a plain program's by a relative error of at most 0.0029.
Values may be sent and summed in bfloat16 or wider, within the bound.
No kernel may reach another device: no remote copies, remote signals or barrier semaphores. Data moves between devices by JAX's collectives and lax.ppermute only.
A program may use at most 64 MiB of HBM per device.

v0:
```python
import math

import jax
import jax.numpy as jnp
from jax import lax
from jax.sharding import PartitionSpec as P


def padded_2(value, sides, width):
    edges = {}
    for axis, dim in sides:
        devices, length = (lax.axis_size(axis), value.shape[dim])
        up = [(i, (i + 1) % devices) for i in range(devices - 1)]
        last = lax.slice_in_dim(value, length - width, length, axis=dim)
        initial = lax.slice_in_dim(value, 0, width, axis=dim)
        edges[dim] = (
            lax.ppermute(last, axis, up),
            lax.ppermute(initial, axis, [(b, a) for a, b in up]),
        )
    done = []
    for _, dim in sides:
        low, high = edges[dim]
        around = [(width, width) if d in done else (0, 0) for d in range(value.ndim)]
        value = jnp.concatenate([jnp.pad(low, around), value, jnp.pad(high, around)], axis=dim)
        done.append(dim)
    return value


def in_blocks(value, dim, devices):
    shape = value.shape
    pieces = value.reshape(*shape[:dim], devices, shape[dim] // devices, *shape[dim + 1 :])
    return jnp.moveaxis(pieces, dim, 0)


def sent_and_summed(value, axis, dim):
    pieces = in_blocks(value, dim, lax.axis_size(axis))
    arrived = lax.all_to_all(pieces, axis, split_axis=0, concat_axis=0, tiled=True)
    return arrived.sum(axis=0)


def rows_for(lines, devices):
    spare = -lines.shape[0] % devices
    if not spare:
        return lines
    return jnp.concatenate([lines, jnp.zeros((spare, *lines.shape[1:]), lines.dtype)])


def total_of(value, axis):
    lines = value.reshape(-1, *value.shape[1:][-1:])
    own = lax.psum_scatter(
        rows_for(lines, lax.axis_size(axis)), axis, scatter_dimension=0, tiled=True
    )
    whole = lax.all_gather(own, axis).reshape(-1, *lines.shape[1:])
    return lax.slice_in_dim(whole, 0, len(lines)).reshape(value.shape)


def from_everyone(value, axis):
    devices = lax.axis_size(axis)
    return lax.all_to_all(
        jnp.broadcast_to(value[None], (devices, *value.shape)), axis, 0, 0, tiled=True
    )


def of_everyone(value, axis):
    return from_everyone(value, axis).sum(axis=0)


def gathered_total(value, axis):
    pieces = lax.all_gather(value, axis)
    return pieces.sum(axis=0)


def on_device(field, previous, kappa, rates, speeds, basis_x, basis_y):
    species, depth, width_x, width_y = field.shape
    rank = basis_x.shape[1]
    row_count = lax.axis_size("row")
    col_count = lax.axis_size("col")
    grp_count = lax.axis_size("grp")
    part_y = width_y // row_count
    grid_x = width_x * row_count
    grid_y = width_y * col_count
    grid_z = depth * grp_count
    padded = padded_2(field, (("grp", 1), ("row", 2), ("col", 3)), 1)
    z_next = padded[:, 2:, 1:-1, 1:-1]
    z_prev = padded[:, :-2, 1:-1, 1:-1]
    x_next = padded[:, 1:-1, 2:, 1:-1]
    x_prev = padded[:, 1:-1, :-2, 1:-1]
    y_next = padded[:, 1:-1, 1:-1, 2:]
    y_prev = padded[:, 1:-1, 1:-1, :-2]
    laplace = z_next + z_prev + x_next + x_prev + y_next + y_prev - 6.0 * field
    speed_z = speeds[:, 0][:, None, None, None]
    speed_x = speeds[:, 1][:, None, None, None]
    speed_y = speeds[:, 2][:, None, None, None]
    transport = (
        speed_z * (z_next - z_prev) + speed_x * (x_next - x_prev) + speed_y * (y_next - y_prev)
    )
    advanced = field + kappa[None] * rates[:, None, None, None] * laplace - 0.5 * transport
    scale_x = math.sqrt(grid_x) / (species * grid_z * grid_y)
    scale_y = math.sqrt(grid_y) / (species * grid_z * rank)
    relaid = lax.all_to_all(previous, "row", split_axis=3, concat_axis=2, tiled=True)
    projected = jnp.einsum(
        "szxy,xr->yszr", relaid, basis_x, preferred_element_type=jnp.float32
    ).astype(jnp.bfloat16)
    local_x = sent_and_summed(
        scale_x
        * jnp.einsum("szxy,yszr->xr", relaid, projected, preferred_element_type=jnp.float32),
        "row",
        0,
    )
    y_start = lax.axis_index("col") * width_y + lax.axis_index("row") * part_y
    rows_y = lax.dynamic_slice_in_dim(basis_y, y_start, part_y, 0)
    core_part = jnp.einsum("yszr,yq->szrq", projected, rows_y, preferred_element_type=jnp.float32)
    core = total_of(core_part, ("row", "col"))
    core_low = core.astype(jnp.bfloat16)
    local_y = scale_y * jnp.einsum(
        "yszr,szrq->yq", projected, core_low, preferred_element_type=jnp.float32
    )
    gram_y = of_everyone(local_y, "grp")
    gram_x = gathered_total(local_x, ("grp", "col"))
    return (advanced, core, gram_x, gram_y)


def solution(mesh):
    return jax.shard_map(
        on_device,
        mesh=mesh,
        in_specs=(
            P(None, "grp", "row", "col"),
            P(None, "grp", "row", "col"),
            P("grp", "row", "col"),
            P(),
            P(),
            P(),
            P(),
        ),
        out_specs=(
            P(None, "grp", "row", "col"),
            P(None, "grp", None, None),
            P("row", None),
            P(("col", "row"), None),
        ),
        check_vma=False,
    )
```

profile of v0, /device:TPU:57, one launch (start us, length us, event | category | flops | bytes accessed | tf_op | source)
XLA Modules:
  0.0 828.7 jit_solution(889327186693480552)
XLA Ops:
  8.9 43.0 %all_to_all.25 = bf16[8,1,128,384]{2,0,1,3:T(8,128)(2,1)S(1)} all-to-all(bf16[8,1,128,384]{2,0,1,3:T(8,128)(2,1)S(1)} %copy.31), channel_id=1, replica_groups=mesh['grp'=8,'row'=24,'col'=4] {'row'}, dimensions={3} | all-to-all | bytes 1572864 | tf_op jit(solution)/shard_map/all_to_all | solution.py:100
  53.6 62.9 %all_to_all.26 = f32[24,128,128]{1,2,0:T(8,128)} all-to-all(f32[24,128,128]{1,2,0:T(8,128)S(1)} %bitcast.71), channel_id=1, replica_groups=mesh['grp'=8,'row'=24,'col'=4] {'row'}, dimensions={0} | all-to-all | bytes 3145728 | tf_op jit(solution)/shard_map/all_to_all | solution.py:37
  116.5 2.2 reduce_sum.27
  118.8 7.2 collective-permute-start
  127.3 3.2 collective-permute-start.2
  130.5 2.1 collective-permute-start.3
  133.6 227.5 %fusion = f32[16,128]{1,0:T(8,128)S(1)} fusion(f32[1056,128]{1,0:T(8,128)S(1)} %concatenate.28), kind=kCustom, calls=%all-reduce-scatter | all-reduce-scatter fusion | flops 196609 | bytes 552960
  363.1 1.9 collective-permute-start.33
  367.0 1.9 collective-permute-start.31
  370.9 9.7 %collective-permute-done.35 = f32[11,128]{1,0:T(8,128)S(1)} collective-permute-done((f32[11,128]{1,0:T(8,128)S(1)}, f32[11,128]{1,0:T(8,128)S(1)}, u32[]{:S(2)}, u32[]{:S(2)}) %collective-permute-start.35) | collective-permute-done | bytes 5664
  382.5 7.2 collective-permute-start.29
  389.7 2.5 collective-permute-start.28
  392.3 4.1 collective-permute-start.27
  401.3 1.9 collective-permute-start.24
  403.3 2.7 collective-permute-start.23
  416.5 1.9 collective-permute-start.19
  422.4 1.9 collective-permute-start.16
  424.3 2.7 constant_dynamic-update-slice_fusion.2
  430.8 1.9 collective-permute-start.13
  432.8 3.7 collective-permute-start.12
  436.5 2.2 collective-permute-start.11
  443.9 3.1 collective-permute-start.8
  447.0 66.6 %collective-permute-start.7 = (f32[16,128]{1,0:T(8,128)S(1)}, f32[16,128]{1,0:T(8,128)S(1)}, u32[]{:S(2)}, u32[]{:S(2)}) collective-permute-start(f32[16,128]{1,0:T(8,128)S(1)} %fusion), channel_id=1, source_target_pairs={{0,2},{1,3},{2,4},{3,5},{4,6},{5,7},{6,8},{7,9},{8,10},{9,11},{10,... | collective-permute-start | bytes 24584
  513.6 20.5 %collective-permute-start.6 = (f32[16,128]{1,0:T(8,128)S(1)}, f32[16,128]{1,0:T(8,128)S(1)}, u32[]{:S(2)}, u32[]{:S(2)}) collective-permute-start(f32[16,128]{1,0:T(8,128)S(1)} %fusion), channel_id=1, source_target_pairs={{0,1},{1,2},{2,3},{3,4},{4,5},{5,6},{6,7},{7,8},{8,9},{9,10},{10,1... | collective-permute-start | bytes 24584
  534.1 2.7 constant_dynamic-update-slice_fusion
  536.8 3.1 collective-permute-start.5
  541.3 5.1 collective-permute-done.6
  546.4 3.3 concatenate.29
  549.7 211.0 %all-gather.2 = f32[96,11,128]{2,1,0:T(8,128)} all-gather(f32[1,11,128]{2,1,0:T(8,128)S(1)} %dynamic-slice_bitcast_fusion), channel_id=2, replica_groups=mesh['grp'=8,'row'=24,'col'=4] {'row','col'}, dimensions={0}, use_global_device_ids=true | all-gather | bytes 546304 | tf_op jit(solution)/shard_map/all_gather | solution.py:53
  762.7 48.5 %all-to-all-start.2 = ((f32[8,16,128]{2,1,0:T(8,128)}), f32[8,16,128]{2,1,0:T(8,128)S(1)}, u32[]{:S(2)}, u32[]{:S(2)}) async-start(f32[8,16,128]{2,1,0:T(8,128)} %broadcast_in_dim.2), calls=%async_computation.2 | async-start | bytes 131072 | tf_op jit(solution)/shard_map/all_to_all | solution.py:59
  811.3 6.2 multiply_subtract_fusion
  818.9 2.0 copy.42
  (89 shorter events, 46.6 us)
Async XLA Ops:
  7.2 811.7 %all-gather.5.cloned.1.call-start = ((), (), s32[]{:S(2)}) async-start(), calls=%async_computation.3 | async-start | bytes 2162688 | tf_op jit(solution)/shard_map/all_gather | solution.py:69
  118.8 248.2 %collective-permute-start = (f32[8,1,128,384]{3,2,1,0:T(8,128)S(1)}, f32[8,1,128,384]{3,2,1,0:T(8,128)}, u32[]{:S(2)}, u32[]{:S(2)}) collective-permute-start(f32[8,1,128,384]{3,2,1,0:T(8,128)S(1)} %copy-done.1), channel_id=1, source_target_pairs={{96,0},{192,96},{288,192},{384,288},{480,384},{576,480},{672,576},... | collective-permute-start | bytes 4718600 | tf_op jit(solution)/shard_map/ppermute | solution.py:18
  126.0 242.9 %collective-permute-start.1 = (f32[8,1,128,384]{3,2,1,0:T(8,128)S(1)}, f32[8,1,128,384]{3,2,1,0:T(8,128)}, u32[]{:S(2)}, u32[]{:S(2)}) collective-permute-start(f32[8,1,128,384]{3,2,1,0:T(8,128)S(1)} %copy-done.1), channel_id=1, source_target_pairs={{0,96},{96,192},{192,288},{288,384},{384,480},{480,576},{576,672},... | collective-permute-start | bytes 4718600 | tf_op jit(solution)/shard_map/ppermute | solution.py:17
  127.3 235.8 %collective-permute-start.2 = (f32[8,1,1,384]{3,2,1,0:T(1,128)S(1)}, f32[8,1,1,384]{3,2,1,0:T(1,128)S(1)}, u32[]{:S(2)}, u32[]{:S(2)}) collective-permute-start(f32[8,1,1,384]{3,2,1,0:T(1,128)S(1)} %get-tuple-element.23), channel_id=1, source_target_pairs={{4,0},{8,4},{12,8},{16,12},{20,16},{24,20},{28,24},{32,28},{36,32}... | collective-permute-start | bytes 36872 | tf_op jit(solution)/shard_map/ppermute | solution.py:18
  130.5 234.5 %collective-permute-start.3 = (f32[8,1,1,384]{3,2,1,0:T(1,128)S(1)}, f32[8,1,1,384]{3,2,1,0:T(1,128)S(1)}, u32[]{:S(2)}, u32[]{:S(2)}) collective-permute-start(f32[8,1,1,384]{3,2,1,0:T(1,128)S(1)} %get-tuple-element.22), channel_id=1, source_target_pairs={{0,4},{4,8},{8,12},{12,16},{16,20},{20,24},{24,28},{28,32},{32,36}... | collective-permute-start | bytes 36872 | tf_op jit(solution)/shard_map/ppermute | solution.py:17
  361.2 21.3 %collective-permute-start.34 = (f32[16,128]{1,0:T(8,128)S(1)}, f32[16,128]{1,0:T(8,128)S(1)}, u32[]{:S(2)}, u32[]{:S(2)}) collective-permute-start(f32[16,128]{1,0:T(8,128)S(1)} %fusion), channel_id=1, source_target_pairs={{0,29},{1,30},{2,31},{3,32},{4,33},{5,34},{6,35},{7,36},{8,37},{9,... | collective-permute-start | bytes 24584
  363.1 26.6 %collective-permute-start.33 = (f32[16,128]{1,0:T(8,128)S(1)}, f32[16,128]{1,0:T(8,128)S(1)}, u32[]{:S(2)}, u32[]{:S(2)}) collective-permute-start(f32[16,128]{1,0:T(8,128)S(1)} %fusion), channel_id=1, source_target_pairs={{0,28},{1,29},{2,30},{3,31},{4,32},{5,33},{6,34},{7,35},{8,36},{9,... | collective-permute-start | bytes 24584
  365.0 27.2 %collective-permute-start.32 = (f32[16,128]{1,0:T(8,128)S(1)}, f32[16,128]{1,0:T(8,128)S(1)}, u32[]{:S(2)}, u32[]{:S(2)}) collective-permute-start(f32[16,128]{1,0:T(8,128)S(1)} %fusion), channel_id=1, source_target_pairs={{0,27},{1,28},{2,29},{3,30},{4,31},{5,32},{6,33},{7,34},{8,35},{9,... | collective-permute-start | bytes 24584
  367.0 29.4 %collective-permute-start.31 = (f32[16,128]{1,0:T(8,128)S(1)}, f32[16,128]{1,0:T(8,128)S(1)}, u32[]{:S(2)}, u32[]{:S(2)}) collective-permute-start(f32[16,128]{1,0:T(8,128)S(1)} %fusion), channel_id=1, source_target_pairs={{0,26},{1,27},{2,28},{3,29},{4,30},{5,31},{6,32},{7,33},{8,34},{9,... | collective-permute-start | bytes 24584
  380.5 18.9 %collective-permute-start.30 = (f32[16,128]{1,0:T(8,128)S(1)}, f32[16,128]{1,0:T(8,128)S(1)}, u32[]{:S(2)}, u32[]{:S(2)}) collective-permute-start(f32[16,128]{1,0:T(8,128)S(1)} %fusion), channel_id=1, source_target_pairs={{0,25},{1,26},{2,27},{3,28},{4,29},{5,30},{6,31},{7,32},{8,33},{9,... | collective-permute-start | bytes 24584
  382.5 18.9 %collective-permute-start.29 = (f32[16,128]{1,0:T(8,128)S(1)}, f32[16,128]{1,0:T(8,128)S(1)}, u32[]{:S(2)}, u32[]{:S(2)}) collective-permute-start(f32[16,128]{1,0:T(8,128)S(1)} %fusion), channel_id=1, source_target_pairs={{0,24},{1,25},{2,26},{3,27},{4,28},{5,29},{6,30},{7,31},{8,32},{9,... | collective-permute-start | bytes 24584
  389.7 13.6 %collective-permute-start.28 = (f32[16,128]{1,0:T(8,128)S(1)}, f32[16,128]{1,0:T(8,128)S(1)}, u32[]{:S(2)}, u32[]{:S(2)}) collective-permute-start(f32[16,128]{1,0:T(8,128)S(1)} %fusion), channel_id=1, source_target_pairs={{0,23},{1,24},{2,25},{3,26},{4,27},{5,28},{6,29},{7,30},{8,31},{9,... | collective-permute-start | bytes 24584
  392.3 14.0 %collective-permute-start.27 = (f32[16,128]{1,0:T(8,128)S(1)}, f32[16,128]{1,0:T(8,128)S(1)}, u32[]{:S(2)}, u32[]{:S(2)}) collective-permute-start(f32[16,128]{1,0:T(8,128)S(1)} %fusion), channel_id=1, source_target_pairs={{0,22},{1,23},{2,24},{3,25},{4,26},{5,27},{6,28},{7,29},{8,30},{9,... | collective-permute-start | bytes 24584
  396.4 13.7 %collective-permute-start.26 = (f32[16,128]{1,0:T(8,128)S(1)}, f32[16,128]{1,0:T(8,128)S(1)}, u32[]{:S(2)}, u32[]{:S(2)}) collective-permute-start(f32[16,128]{1,0:T(8,128)S(1)} %fusion), channel_id=1, source_target_pairs={{0,21},{1,22},{2,23},{3,24},{4,25},{5,26},{6,27},{7,28},{8,29},{9,... | collective-permute-start | bytes 24584
  399.4 15.2 %collective-permute-start.25 = (f32[16,128]{1,0:T(8,128)S(1)}, f32[16,128]{1,0:T(8,128)S(1)}, u32[]{:S(2)}, u32[]{:S(2)}) collective-permute-start(f32[16,128]{1,0:T(8,128)S(1)} %fusion), channel_id=1, source_target_pairs={{0,20},{1,21},{2,22},{3,23},{4,24},{5,25},{6,26},{7,27},{8,28},{9,... | collective-permute-start | bytes 24584
  401.3 15.2 %collective-permute-start.24 = (f32[16,128]{1,0:T(8,128)S(1)}, f32[16,128]{1,0:T(8,128)S(1)}, u32[]{:S(2)}, u32[]{:S(2)}) collective-permute-start(f32[16,128]{1,0:T(8,128)S(1)} %fusion), channel_id=1, source_target_pairs={{0,19},{1,20},{2,21},{3,22},{4,23},{5,24},{6,25},{7,26},{8,27},{9,... | collective-permute-start | bytes 24584
  403.3 15.2 %collective-permute-start.23 = (f32[16,128]{1,0:T(8,128)S(1)}, f32[16,128]{1,0:T(8,128)S(1)}, u32[]{:S(2)}, u32[]{:S(2)}) collective-permute-start(f32[16,128]{1,0:T(8,128)S(1)} %fusion), channel_id=1, source_target_pairs={{0,18},{1,19},{2,20},{3,21},{4,22},{5,23},{6,24},{7,25},{8,26},{9,... | collective-permute-start | bytes 24584
  406.3 14.1 %collective-permute-start.22 = (f32[16,128]{1,0:T(8,128)S(1)}, f32[16,128]{1,0:T(8,128)S(1)}, u32[]{:S(2)}, u32[]{:S(2)}) collective-permute-start(f32[16,128]{1,0:T(8,128)S(1)} %fusion), channel_id=1, source_target_pairs={{0,17},{1,18},{2,19},{3,20},{4,21},{5,22},{6,23},{7,24},{8,25},{9,... | collective-permute-start | bytes 24584
  422.4 14.2 %collective-permute-start.16 = (f32[16,128]{1,0:T(8,128)S(1)}, f32[16,128]{1,0:T(8,128)S(1)}, u32[]{:S(2)}, u32[]{:S(2)}) collective-permute-start(f32[16,128]{1,0:T(8,128)S(1)} %fusion), channel_id=1, source_target_pairs={{0,11},{1,12},{2,13},{3,14},{4,15},{5,16},{6,17},{7,18},{8,19},{9,... | collective-permute-start | bytes 24584
  426.9 13.1 %collective-permute-start.15 = (f32[16,128]{1,0:T(8,128)S(1)}, f32[16,128]{1,0:T(8,128)S(1)}, u32[]{:S(2)}, u32[]{:S(2)}) collective-permute-start(f32[16,128]{1,0:T(8,128)S(1)} %fusion), channel_id=1, source_target_pairs={{0,10},{1,11},{2,12},{3,13},{4,14},{5,15},{6,16},{7,17},{8,18},{9,... | collective-permute-start | bytes 24584
  428.9 13.1 %collective-permute-start.14 = (f32[16,128]{1,0:T(8,128)S(1)}, f32[16,128]{1,0:T(8,128)S(1)}, u32[]{:S(2)}, u32[]{:S(2)}) collective-permute-start(f32[16,128]{1,0:T(8,128)S(1)} %fusion), channel_id=1, source_target_pairs={{0,9},{1,10},{2,11},{3,12},{4,13},{5,14},{6,15},{7,16},{8,17},{9,1... | collective-permute-start | bytes 24584
  430.8 13.1 %collective-permute-start.13 = (f32[16,128]{1,0:T(8,128)S(1)}, f32[16,128]{1,0:T(8,128)S(1)}, u32[]{:S(2)}, u32[]{:S(2)}) collective-permute-start(f32[16,128]{1,0:T(8,128)S(1)} %fusion), channel_id=1, source_target_pairs={{0,8},{1,9},{2,10},{3,11},{4,12},{5,13},{6,14},{7,15},{8,16},{9,17... | collective-permute-start | bytes 24584
  432.8 14.2 %collective-permute-start.12 = (f32[16,128]{1,0:T(8,128)S(1)}, f32[16,128]{1,0:T(8,128)S(1)}, u32[]{:S(2)}, u32[]{:S(2)}) collective-permute-start(f32[16,128]{1,0:T(8,128)S(1)} %fusion), channel_id=1, source_target_pairs={{0,7},{1,8},{2,9},{3,10},{4,11},{5,12},{6,13},{7,14},{8,15},{9,16}... | collective-permute-start | bytes 24584
  436.5 77.1 %collective-permute-start.11 = (f32[16,128]{1,0:T(8,128)S(1)}, f32[16,128]{1,0:T(8,128)S(1)}, u32[]{:S(2)}, u32[]{:S(2)}) collective-permute-start(f32[16,128]{1,0:T(8,128)S(1)} %fusion), channel_id=1, source_target_pairs={{0,6},{1,7},{2,8},{3,9},{4,10},{5,11},{6,12},{7,13},{8,14},{9,15},... | collective-permute-start | bytes 24584
  440.0 96.8 %collective-permute-start.10 = (f32[16,128]{1,0:T(8,128)S(1)}, f32[16,128]{1,0:T(8,128)S(1)}, u32[]{:S(2)}, u32[]{:S(2)}) collective-permute-start(f32[16,128]{1,0:T(8,128)S(1)} %fusion), channel_id=1, source_target_pairs={{0,5},{1,6},{2,7},{3,8},{4,9},{5,10},{6,11},{7,12},{8,13},{9,14},{... | collective-permute-start | bytes 24584
  442.0 98.0 %collective-permute-start.9 = (f32[16,128]{1,0:T(8,128)S(1)}, f32[16,128]{1,0:T(8,128)S(1)}, u32[]{:S(2)}, u32[]{:S(2)}) collective-permute-start(f32[16,128]{1,0:T(8,128)S(1)} %fusion), channel_id=1, source_target_pairs={{0,4},{1,5},{2,6},{3,7},{4,8},{5,9},{6,10},{7,11},{8,12},{9,13},{1... | collective-permute-start | bytes 24584
  443.9 97.4 %collective-permute-start.8 = (f32[16,128]{1,0:T(8,128)S(1)}, f32[16,128]{1,0:T(8,128)S(1)}, u32[]{:S(2)}, u32[]{:S(2)}) collective-permute-start(f32[16,128]{1,0:T(8,128)S(1)} %fusion), channel_id=1, source_target_pairs={{0,3},{1,4},{2,5},{3,6},{4,7},{5,8},{6,9},{7,10},{8,11},{9,12},{10... | collective-permute-start | bytes 24584
  447.0 94.3 %collective-permute-start.7 = (f32[16,128]{1,0:T(8,128)S(1)}, f32[16,128]{1,0:T(8,128)S(1)}, u32[]{:S(2)}, u32[]{:S(2)}) collective-permute-start(f32[16,128]{1,0:T(8,128)S(1)} %fusion), channel_id=1, source_target_pairs={{0,2},{1,3},{2,4},{3,5},{4,6},{5,7},{6,8},{7,9},{8,10},{9,11},{10,... | collective-permute-start | bytes 24584
  513.6 32.8 %collective-permute-start.6 = (f32[16,128]{1,0:T(8,128)S(1)}, f32[16,128]{1,0:T(8,128)S(1)}, u32[]{:S(2)}, u32[]{:S(2)}) collective-permute-start(f32[16,128]{1,0:T(8,128)S(1)} %fusion), channel_id=1, source_target_pairs={{0,1},{1,2},{2,3},{3,4},{4,5},{5,6},{6,7},{7,8},{8,9},{9,10},{10,1... | collective-permute-start | bytes 24584
  536.8 274.5 %collective-permute-start.5 = (f32[8,1,128,1]{3,2,1,0:T(8,128)}, f32[8,1,128,1]{3,2,1,0:T(8,128)S(1)}, u32[]{:S(2)}, u32[]{:S(2)}) collective-permute-start(f32[8,1,128,1]{3,2,1,0:T(8,128)} %get-tuple-element.21), channel_id=1, source_target_pairs={{0,1},{1,2},{2,3},{4,5},{5,6},{6,7},{8,9},{9,10},{10,11},{12,13},{... | collective-permute-start | bytes 12296 | tf_op jit(solution)/shard_map/ppermute | solution.py:17
  540.0 271.3 %collective-permute-start.4 = (f32[8,1,128,1]{3,2,1,0:T(8,128)}, f32[8,1,128,1]{3,2,1,0:T(8,128)}, u32[]{:S(2)}, u32[]{:S(2)}) collective-permute-start(f32[8,1,128,1]{3,2,1,0:T(8,128)} %get-tuple-element.20), channel_id=1, source_target_pairs={{1,0},{2,1},{3,2},{5,4},{6,5},{7,6},{9,8},{10,9},{11,10},{13,12},{... | collective-permute-start | bytes 12296 | tf_op jit(solution)/shard_map/ppermute | solution.py:18
  762.7 55.5 %all-to-all-start.2 = ((f32[8,16,128]{2,1,0:T(8,128)}), f32[8,16,128]{2,1,0:T(8,128)S(1)}, u32[]{:S(2)}, u32[]{:S(2)}) async-start(f32[8,16,128]{2,1,0:T(8,128)} %broadcast_in_dim.2), calls=%async_computation.2 | async-start | bytes 131072 | tf_op jit(solution)/shard_map/all_to_all | solution.py:59
  (10 other events, 660.9 us)
Sparse Core Ops, SparseCore 0:
  118.9 77.1 all-gather.4
where the time goes:
time: 830 us; the launch traced here: 829 us
  blocking collectives  544 us (66%)
  starting transfers between devices  220 us (27%)
  local copies, waits for them, and re-layouts  21 us (3%)
  waiting for transfers between devices  17.1 us (2%)
  between operations  15.4 us (2%)
  other arithmetic  9.23 us (1%)
    unnamed x1, blocking collectives  228 us
    all_gather x1, blocking collectives, total_of(): whole = lax.all_gather(own, axis).reshape(-1, *lines.shape[1:])  211 us
    unnamed x30, starting transfers between devices  153 us
    all_to_all x1, blocking collectives, sent_and_summed(): lax.all_to_all(pieces, axis, split_axis=0, concat_axis=0, tiled=True)  62.9 us
    all_to_all x1, starting transfers between devices, from_everyone(): lax.all_to_all(jnp.broadcast_to(value[None], (devices, *value.shape)), ax...  48.5 us
    all_to_all x1, blocking collectives, on_device(): lax.all_to_all(previous, 'row', split_axis=3, concat_axis=2, tiled=True)  43 us
    unnamed x31, waiting for transfers between devices  17.1 us
  transfers between devices with their start and end apart: 38, of which 4 were waited for; matrix products, arithmetic and copies ran while one was open for 30% of the time, Pallas kernels for 0%

commit v1 on v0

v1 whole, which is shorter than its diff:
```python
import math

import jax
import jax.numpy as jnp
from jax import lax
from jax.sharding import Mesh
from jax.sharding import PartitionSpec as P

F32 = jnp.float32
BF16 = jnp.bfloat16
GRP = ("yh", "core")
ROW = ("yl", "zh", "zl")
QUAD = ("yl", "zl")


def chain(n):
    return [(i, i + 1) for i in range(n - 1)]


def back(n):
    return [(i + 1, i) for i in range(n - 1)]


def exchanged(value, axes):
    return lax.all_to_all(value, axes, 0, 0, tiled=True)


def dot(a, b, dims):
    return lax.dot_general(a, b, dims, preferred_element_type=F32)


def stencil(field, kappa, rates, speeds):
    u = field[:, 0]
    n_grp, n_row, n_col = lax.axis_size(GRP), lax.axis_size(ROW), lax.axis_size("x")
    low = u.astype(BF16)
    z_prev = lax.ppermute(low, GRP, chain(n_grp)).astype(F32)
    z_next = lax.ppermute(low, GRP, back(n_grp)).astype(F32)
    x_low = lax.ppermute(u[:, -1, :], ROW, chain(n_row))
    x_high = lax.ppermute(u[:, 0, :], ROW, back(n_row))
    y_low = lax.ppermute(u[:, :, -1], "x", chain(n_col))
    y_high = lax.ppermute(u[:, :, 0], "x", back(n_col))
    x_prev = jnp.concatenate([x_low[:, None, :], u[:, :-1, :]], axis=1)
    x_next = jnp.concatenate([u[:, 1:, :], x_high[:, None, :]], axis=1)
    y_prev = jnp.concatenate([y_low[:, :, None], u[:, :, :-1]], axis=2)
    y_next = jnp.concatenate([u[:, :, 1:], y_high[:, :, None]], axis=2)
    laplace = z_next + z_prev + x_next + x_prev + y_next + y_prev - 6.0 * u
    sz, sx, sy = (speeds[:, d][:, None, None] for d in range(3))
    transport = sz * (z_next - z_prev) + sx * (x_next - x_prev) + sy * (y_next - y_prev)
    out = u + kappa * rates[:, None, None] * laplace - 0.5 * transport
    return out[:, None]


def on_device(field, previous, kappa, rates, speeds, basis_x, basis_y):
    species, depth, width_x, width_y = field.shape
    rank = basis_x.shape[1]
    n_quad, n_zh, n_col = lax.axis_size(QUAD), lax.axis_size("zh"), lax.axis_size("x")
    n_grp, n_row = lax.axis_size(GRP), lax.axis_size(ROW)
    own = species // n_quad
    grid_x, grid_y, grid_z = width_x * n_row, width_y * n_col, depth * n_grp
    part_y = width_y // n_row
    scale_x = math.sqrt(grid_x) / (species * grid_z * grid_y)
    scale_y = math.sqrt(grid_y) / (species * grid_z * rank)
    zh = lax.axis_index("zh")

    advanced = stencil(field, kappa, rates, speeds)

    lines = exchanged(previous.reshape(n_quad, own, width_x, width_y), QUAD)
    bx = basis_x.reshape(lax.axis_size("yl"), n_zh, lax.axis_size("zl"), width_x, rank)
    bx = lax.dynamic_index_in_dim(bx, zh, 1, keepdims=False).reshape(n_quad, width_x, rank)
    partial = sum(
        dot(lines[j], bx[j], (((1,), (0,)), ((), ()))) for j in range(n_quad)
    )
    pieces = partial.reshape(n_zh, own * width_y // n_zh, rank)
    mine = exchanged(pieces, "zh").sum(axis=0).astype(BF16)
    projected = lax.all_gather(mine, "zh", tiled=True).reshape(own, width_y, rank)

    by = lax.dynamic_slice_in_dim(basis_y, lax.axis_index("x") * width_y, width_y, 0)
    core_part = dot(projected, by, (((1,), (0,)), ((), ())))
    core_own = lax.all_gather(core_part, "x").sum(axis=0)
    core = lax.all_gather(core_own, QUAD, tiled=True)[:, None]

    gx = jnp.stack(
        [
            sum(
                dot(lines[j, s], projected[s], (((1,), (0,)), ((), ())))
                for s in range(own)
            )
            for j in range(n_quad)
        ]
    )
    gx = exchanged(scale_x * gx, QUAD).sum(axis=0)
    gx = lax.all_gather(gx, "x").sum(axis=0)
    gram_x = lax.all_gather(gx, GRP).sum(axis=0)

    half = part_y * lax.axis_size("zl")
    rows = projected.reshape(own, lax.axis_size("yl"), n_zh, half, rank)
    rows = lax.dynamic_index_in_dim(rows, zh, 2, keepdims=False)
    rows = rows.reshape(own, n_quad * part_y, rank)
    core_low = core_own.astype(BF16)
    gy = scale_y * sum(dot(rows[s], core_low[s], (((1,), (0,)), ((), ()))) for s in range(own))
    gy = exchanged(gy.reshape(n_quad, part_y, rank), QUAD).sum(axis=0)
    gram_y = lax.all_gather(gy, GRP).sum(axis=0)
    return (advanced, core, gram_x, gram_y)


def solution(mesh):
    split = Mesh(
        mesh.devices.reshape(4, 2, 2, 6, 2, 4), ("yh", "core", "yl", "zh", "zl", "x")
    )
    block = P(None, GRP, ROW, "x")
    return jax.shard_map(
        on_device,
        mesh=split,
        in_specs=(block, block, P(GRP, ROW, "x"), P(), P(), P(), P()),
        out_specs=(block, P(None, GRP, None, None), P(ROW, None), P(("x", *ROW), None)),
        check_vma=False,
    )
```

time: 830 us -> 178 us (0.21)
  blocking collectives: 544 us -> 97.1 us
  starting transfers between devices: 220 us -> 45.4 us
  waiting for transfers between devices: 17.1 us -> 0.35 us
  between operations: 15.4 us -> 1 us
    unnamed x1 -> x0, blocking collectives: 228 us -> none
    unnamed x30 -> x0, starting transfers between devices: 153 us -> none
    all_gather x1 -> x6, blocking collectives: 211 us -> 97.1 us  [the longest x1 28 us: on_device(): gram_y = lax.all_gather(gy, GRP).sum(axis=0)]
    all_to_all x2 -> x0, blocking collectives: 106 us -> none  [the longest x1 62.9 us: sent_and_summed(): lax.all_to_all(pieces, axis, split_axis=0, concat_axis=0, tiled=True)]
    all_to_all x1 -> x4, starting transfers between devices: 48.5 us -> 27.7 us  [exchanged(): return lax.all_to_all(value, axes, 0, 0, tiled=True)]
    unnamed x31 -> x0, waiting for transfers between devices: 17.1 us -> none
  transfers between devices with their start and end apart: 38 -> 10, of which waited for: 4 -> 1; matrix products, arithmetic and copies ran while one was open for 30% -> 17% of each run, Pallas kernels for 0% -> 0%
where the time goes in v1:
time: 178 us; the launch traced here: 176 us
  blocking collectives  97.1 us (55%)
  starting transfers between devices  45.4 us (26%)
  local copies, waits for them, and re-layouts  19.8 us (11%)
  other arithmetic  7.03 us (4%)
  matrix products  5.2 us (3%)
    all_gather x1, blocking collectives, on_device(): gram_y = lax.all_gather(gy, GRP).sum(axis=0)  28 us
    all_to_all x4, starting transfers between devices, exchanged(): return lax.all_to_all(value, axes, 0, 0, tiled=True)  27.7 us
    all_gather x1, blocking collectives, on_device(): gram_x = lax.all_gather(gx, GRP).sum(axis=0)  18.4 us
    all_gather x1, blocking collectives, on_device(): lax.all_gather(mine, 'zh', tiled=True).reshape(own, width_y, rank)  18.2 us
    all_gather x1, blocking collectives, on_device(): core_own = lax.all_gather(core_part, 'x').sum(axis=0)  11.5 us
    all_gather x1, blocking collectives, on_device(): core = lax.all_gather(core_own, QUAD, tiled=True)[:, None]  11.1 us
    all_gather x1, blocking collectives, on_device(): gx = lax.all_gather(gx, 'x').sum(axis=0)  9.88 us
    unnamed x27, local copies, waits for them, and re-layouts  6.14 us
  transfers between devices with their start and end apart: 10, of which 1 were waited for; matrix products, arithmetic and copies ran while one was open for 17% of the time, Pallas kernels for 0%

profile of v1, /device:TPU:57, one launch (start us, length us, event | category | flops | bytes accessed | tf_op | source)
XLA Modules:
  0.0 175.9 jit_solution(5200488569725644145)
XLA Ops:
  0.7 4.7 %all-to-all-start = ((bf16[4,2,128,384]{3,2,1,0:T(8,128)(2,1)}), bf16[4,2,128,384]{3,2,1,0:T(8,128)(2,1)S(1)}, u32[]{:S(2)}, u32[]{:S(2)}) async-start(bf16[4,2,128,384]{3,2,1,0:T(8,128)(2,1)} %bitcast.141), calls=%async_computation | async-start | bytes 1572864 | tf_op jit(solution)/shard_map/all_to_all | solution.py:25
  5.3 1.8 %copy.93 = bf16[8,1,128,384]{3,0,2,1:T(8,128)(2,1)} copy(f32[8,1,128,384]{3,2,1,0:T(8,128)S(1)} %copy-done.1) | data formatting | bytes 2359296 | tf_op args[0]
  7.1 1.3 collective-permute-start.1
  8.4 4.7 %collective-permute-start = (bf16[8,128,384]{2,0,1:T(8,128)(2,1)}, bf16[8,128,384]{2,0,1:T(8,128)(2,1)}, u32[]{:S(2)}, u32[]{:S(2)}) collective-permute-start(bf16[8,128,384]{2,0,1:T(8,128)(2,1)} %bitcast.129), channel_id=1, source_target_pairs={{96,0},{192,96},{288,192},{384,288},{480,384},{576,480},{672,576},... | collective-permute-start | bytes 2359304 | tf_op jit(solution)/shard_map/ppermute | solution.py:37
  13.1 0.9 copy.92
  14.0 1.1 fusion.40
  15.1 1.8 %copy.76 = f32[8,128,1]{1,0,2:T(8,128)} copy(f32[8,128,1]{2,0,1:T(8,128)} %get-tuple-element.39) | data formatting | bytes 8192 | tf_op jit(solution)/shard_map/slice | solution.py:40
  16.9 3.1 %collective-permute-start.5 = (f32[8,128]{1,0:T(8,128)}, f32[8,128]{1,0:T(8,128)S(1)}, u32[]{:S(2)}, u32[]{:S(2)}) collective-permute-start(f32[8,128]{1,0:T(8,128)} %bitcast.8), channel_id=1, source_target_pairs={{0,1},{1,2},{2,3},{4,5},{5,6},{6,7},{8,9},{9,10},{10,11},{12,13},{... | collective-permute-start | bytes 12296 | tf_op jit(solution)/shard_map/ppermute | solution.py:40
  20.0 1.8 %copy.74 = f32[8,128,1]{1,0,2:T(8,128)} copy(f32[8,128,1]{2,0,1:T(8,128)} %get-tuple-element.38) | data formatting | bytes 8192 | tf_op jit(solution)/shard_map/slice | solution.py:41
  21.8 1.3 collective-permute-start.4
  24.2 1.0 fusion.13
  25.1 0.9 copy.79
  26.0 13.9 %all-to-all-start.1 = ((f32[6,128,128]{2,1,0:T(8,128)}), f32[6,128,128]{2,1,0:T(8,128)S(1)}, u32[]{:S(2)}, u32[]{:S(2)}) async-start(f32[6,128,128]{2,1,0:T(8,128)} %bitcast.140), calls=%async_computation.1 | async-start | bytes 786432 | tf_op jit(solution)/shard_map/all_to_all | solution.py:25
  40.6 2.5 %collective-permute-start.3 = (f32[8,384]{1,0:T(8,128)}, f32[8,384]{1,0:T(8,128)S(1)}, u32[]{:S(2)}, u32[]{:S(2)}) collective-permute-start(f32[8,384]{1,0:T(8,128)} %get-tuple-element.35), channel_id=1, source_target_pairs={{0,4},{4,8},{8,12},{12,16},{16,20},{20,24},{24,28},{28,32},{32,36}... | collective-permute-start | bytes 36872 | tf_op jit(solution)/shard_map/ppermute | solution.py:38
  43.1 1.8 %fusion.38 = (f32[8,127,384]{2,0,1:T(8,128)}, f32[8,127,384]{2,0,1:T(8,128)}) fusion(f32[8,128,384]{2,0,1:T(8,128)S(1)} %bitcast.133), kind=kLoop, calls=%fused_computation.81 | loop fusion | bytes 6242304 | tf_op jit(solution)/shard_map/slice | solution.py:43
  45.0 2.2 %fusion.39 = (f32[8,128,383]{2,0,1:T(8,128)}, f32[8,128,383]{2,0,1:T(8,128)}) fusion(f32[8,128,384]{2,0,1:T(8,128)S(1)} %bitcast.134), kind=kLoop, calls=%fused_computation.82 | loop fusion | bytes 6275072 | tf_op jit(solution)/shard_map/slice | solution.py:45
  47.6 4.9 %collective-permute-start.2 = (f32[8,384]{1,0:T(8,128)}, f32[8,384]{1,0:T(8,128)}, u32[]{:S(2)}, u32[]{:S(2)}) collective-permute-start(f32[8,384]{1,0:T(8,128)} %get-tuple-element.34), channel_id=1, source_target_pairs={{4,0},{8,4},{12,8},{16,12},{20,16},{24,20},{28,24},{32,28},{36,32}... | collective-permute-start | bytes 36872 | tf_op jit(solution)/shard_map/ppermute | solution.py:39
  52.5 1.0 copy.77
  53.5 1.7 copy.75
  55.3 18.2 %all_gather.30 = bf16[768,128]{1,0:T(8,128)(2,1)S(1)} all-gather(bf16[128,128]{1,0:T(8,128)(2,1)S(1)} %reduce_sum.63), channel_id=1, replica_groups=mesh['yh'=4,'core'=2,'yl'=2,'zh'=6,'zl'=2,'x'=4] {'zh'}, dimensions={0}, use_global_device_ids=true | all-gather | bytes 229376 | tf_op jit(solution)/shard_map/all_gather | solution.py:75
  73.5 1.1 fusion.24
  74.6 11.5 %all-gather = f32[8,128,128]{2,1,0:T(8,128)S(1)} all-gather(f32[2,128,128]{2,1,0:T(8,128)S(1)} %fusion.24), channel_id=2, replica_groups=mesh['yh'=4,'core'=2,'yl'=2,'zh'=6,'zl'=2,'x'=4] {'x'}, dimensions={0}, use_global_device_ids=true | all-gather | bytes 655360 | tf_op jit(solution)/shard_map/all_gather | solution.py:79
  86.3 0.8 fusion.18
  87.1 4.6 %all-to-all-start.3 = ((f32[4,16,128]{2,1,0:T(8,128)}), f32[4,16,128]{2,1,0:T(8,128)S(1)}, u32[]{:S(2)}, u32[]{:S(2)}) async-start(f32[4,16,128]{2,1,0:T(8,128)} %bitcast.57), calls=%async_computation.3 | async-start | bytes 65536 | tf_op jit(solution)/shard_map/all_to_all | solution.py:25
  94.5 4.5 %all-to-all-start.2 = ((f32[4,128,128]{1,2,0:T(8,128)}), f32[4,128,128]{1,2,0:T(8,128)S(1)}, u32[]{:S(2)}, u32[]{:S(2)}) async-start(f32[4,128,128]{1,2,0:T(8,128)} %maximum_multiply_fusion), calls=%async_computation.2 | async-start | bytes 524288 | tf_op jit(solution)/shard_map/all_to_all | solution.py:25
  99.1 5.3 %fusion.8 = f32[8,1,128,384]{3,0,2,1:T(8,128)S(1)} fusion(bf16[8,128,384]{2,0,1:T(8,128)(2,1)} %collective-permute-done.1, bf16[8,128,384]{2,0,1:T(8,128)(2,1)} %collective-permute-done, f32[8,128,383]{2,0,1:T(8,128)} %get-tuple-element.37, f32[8,128,1]{2,0,1:T(8,128)} %copy.77, f32[8,128,1]{2,0,1:T(8,128)} %copy.75, f32[8,128,383]{2,0,1:T(8,128)} %get-tuple-element.36, ...), kind=kLoop, calls=%fused_computation.10 | loop fusion | flops 10223616 | bytes 11206784 | tf_op jit(solution)/shard_map/broadcast_in_dim | solution.py:50
  104.4 1.4 copy.81
  105.8 11.1 %all_gather.33 = f32[8,128,128]{2,1,0:T(8,128)S(1)} all-gather(f32[2,128,128]{2,1,0:T(8,128)S(1)} %reduce_sum.64), channel_id=1, replica_groups=mesh['yh'=4,'core'=2,'yl'=2,'zh'=6,'zl'=2,'x'=4] {'yl','zl'}, dimensions={0}, use_global_device_ids=true | all-gather | bytes 655360 | tf_op jit(solution)/shard_map/all_gather | solution.py:80
  116.9 28.0 %all-gather.3 = f32[128,128]{1,0:T(8,128)S(1)} all-gather(f32[16,128]{1,0:T(8,128)S(1)} %reduce_sum.68), channel_id=5, replica_groups=mesh['yh'=4,'core'=2,'yl'=2,'zh'=6,'zl'=2,'x'=4] {'yh','core'}, dimensions={0}, use_global_device_ids=true | all-gather | bytes 73728 | tf_op jit(solution)/shard_map/all_gather | solution.py:102
  145.6 9.9 %all-gather.1 = f32[512,128]{0,1:T(8,128)S(1)} all-gather(f32[128,128]{0,1:T(8,128)S(1)} %reduce_sum.65), channel_id=3, replica_groups=mesh['yh'=4,'core'=2,'yl'=2,'zh'=6,'zl'=2,'x'=4] {'x'}, dimensions={0}, use_global_device_ids=true | all-gather | bytes 327680 | tf_op jit(solution)/shard_map/all_gather | solution.py:92
  155.7 18.4 %all-gather.2 = f32[1024,128]{0,1:T(8,128)S(1)} all-gather(f32[128,128]{0,1:T(8,128)S(1)} %reduce_sum.66), channel_id=4, replica_groups=mesh['yh'=4,'core'=2,'yl'=2,'zh'=6,'zl'=2,'x'=4] {'yh','core'}, dimensions={0}, use_global_device_ids=true | all-gather | bytes 589824 | tf_op jit(solution)/shard_map/all_gather | solution.py:93
  175.1 0.8 copy.95
  (59 shorter events, 6.9 us)
Async XLA Ops:
  0.6 22.5 %copy-start = (bf16[3072,128]{1,0:T(8,128)(2,1)S(1)}, bf16[3072,128]{1,0:T(8,128)(2,1)}, u32[]{:S(2)}) copy-start(bf16[3072,128]{1,0:T(8,128)(2,1)} %param.12) | copy-start | bytes 2359300
  0.6 4.7 %copy-start.1 = (f32[8,1,128,384]{3,2,1,0:T(8,128)S(1)}, f32[8,1,128,384]{3,2,1,0:T(8,128)}, u32[]{:S(2)}) copy-start(f32[8,1,128,384]{3,2,1,0:T(8,128)} %param.7) | copy-start | bytes 4718596
  0.7 22.7 %all-to-all-start = ((bf16[4,2,128,384]{3,2,1,0:T(8,128)(2,1)}), bf16[4,2,128,384]{3,2,1,0:T(8,128)(2,1)S(1)}, u32[]{:S(2)}, u32[]{:S(2)}) async-start(bf16[4,2,128,384]{3,2,1,0:T(8,128)(2,1)} %bitcast.141), calls=%async_computation | async-start | bytes 1572864 | tf_op jit(solution)/shard_map/all_to_all | solution.py:25
  5.3 7.7 %copy-start.2 = (f32[8,1,128,384]{3,2,1,0:T(8,128)S(1)}, f32[8,1,128,384]{3,2,1,0:T(8,128)}, u32[]{:S(2)}) copy-start(f32[8,1,128,384]{3,2,1,0:T(8,128)} %param.7) | copy-start | bytes 4718596
  7.1 91.9 %collective-permute-start.1 = (bf16[8,128,384]{2,0,1:T(8,128)(2,1)}, bf16[8,128,384]{2,0,1:T(8,128)(2,1)}, u32[]{:S(2)}, u32[]{:S(2)}) collective-permute-start(bf16[8,128,384]{2,0,1:T(8,128)(2,1)} %bitcast.129), channel_id=1, source_target_pairs={{0,96},{96,192},{192,288},{288,384},{384,480},{480,576},{576,672},... | collective-permute-start | bytes 2359304 | tf_op jit(solution)/shard_map/ppermute | solution.py:36
  8.4 90.6 %collective-permute-start = (bf16[8,128,384]{2,0,1:T(8,128)(2,1)}, bf16[8,128,384]{2,0,1:T(8,128)(2,1)}, u32[]{:S(2)}, u32[]{:S(2)}) collective-permute-start(bf16[8,128,384]{2,0,1:T(8,128)(2,1)} %bitcast.129), channel_id=1, source_target_pairs={{96,0},{192,96},{288,192},{384,288},{480,384},{576,480},{672,576},... | collective-permute-start | bytes 2359304 | tf_op jit(solution)/shard_map/ppermute | solution.py:37
  16.9 30.7 %collective-permute-start.5 = (f32[8,128]{1,0:T(8,128)}, f32[8,128]{1,0:T(8,128)S(1)}, u32[]{:S(2)}, u32[]{:S(2)}) collective-permute-start(f32[8,128]{1,0:T(8,128)} %bitcast.8), channel_id=1, source_target_pairs={{0,1},{1,2},{2,3},{4,5},{5,6},{6,7},{8,9},{9,10},{10,11},{12,13},{... | collective-permute-start | bytes 12296 | tf_op jit(solution)/shard_map/ppermute | solution.py:40
  21.8 31.7 %collective-permute-start.4 = (f32[8,128]{1,0:T(8,128)}, f32[8,128]{1,0:T(8,128)}, u32[]{:S(2)}, u32[]{:S(2)}) collective-permute-start(f32[8,128]{1,0:T(8,128)} %bitcast.6), channel_id=1, source_target_pairs={{1,0},{2,1},{3,2},{5,4},{6,5},{7,6},{9,8},{10,9},{11,10},{13,12},{... | collective-permute-start | bytes 12296 | tf_op jit(solution)/shard_map/ppermute | solution.py:41
  23.3 0.7 copy-start.4
  26.0 29.2 %all-to-all-start.1 = ((f32[6,128,128]{2,1,0:T(8,128)}), f32[6,128,128]{2,1,0:T(8,128)S(1)}, u32[]{:S(2)}, u32[]{:S(2)}) async-start(f32[6,128,128]{2,1,0:T(8,128)} %bitcast.140), calls=%async_computation.1 | async-start | bytes 786432 | tf_op jit(solution)/shard_map/all_to_all | solution.py:25
  40.6 58.4 %collective-permute-start.3 = (f32[8,384]{1,0:T(8,128)}, f32[8,384]{1,0:T(8,128)S(1)}, u32[]{:S(2)}, u32[]{:S(2)}) collective-permute-start(f32[8,384]{1,0:T(8,128)} %get-tuple-element.35), channel_id=1, source_target_pairs={{0,4},{4,8},{8,12},{12,16},{16,20},{20,24},{24,28},{28,32},{32,36}... | collective-permute-start | bytes 36872 | tf_op jit(solution)/shard_map/ppermute | solution.py:38
  45.0 2.2 %copy-start.8 = (f32[8,3]{0,1:T(4,128)S(1)}, f32[8,3]{0,1:T(4,128)}, u32[]{:S(2)}) copy-start(f32[8,3]{0,1:T(4,128)} %param.11) | copy-start | bytes 292
  47.6 51.4 %collective-permute-start.2 = (f32[8,384]{1,0:T(8,128)}, f32[8,384]{1,0:T(8,128)}, u32[]{:S(2)}, u32[]{:S(2)}) collective-permute-start(f32[8,384]{1,0:T(8,128)} %get-tuple-element.34), channel_id=1, source_target_pairs={{4,0},{8,4},{12,8},{16,12},{20,16},{24,20},{28,24},{32,28},{36,32}... | collective-permute-start | bytes 36872 | tf_op jit(solution)/shard_map/ppermute | solution.py:39
  87.1 7.4 %all-to-all-start.3 = ((f32[4,16,128]{2,1,0:T(8,128)}), f32[4,16,128]{2,1,0:T(8,128)S(1)}, u32[]{:S(2)}, u32[]{:S(2)}) async-start(f32[4,16,128]{2,1,0:T(8,128)} %bitcast.57), calls=%async_computation.3 | async-start | bytes 65536 | tf_op jit(solution)/shard_map/all_to_all | solution.py:25
  92.0 7.1 %copy-start.3 = (f32[8,1,128,384]{3,2,1,0:T(8,128)S(1)}, f32[8,1,128,384]{3,2,1,0:T(8,128)}, u32[]{:S(2)}) copy-start(f32[8,1,128,384]{3,2,1,0:T(8,128)} %param.7) | copy-start | bytes 4718596
  92.0 7.1 %copy-start.5 = (f32[8]{0:T(128)S(1)}, f32[8]{0:T(128)}, u32[]{:S(2)}) copy-start(f32[8]{0:T(128)} %get-tuple-element.42) | copy-start | bytes 100
  92.0 7.1 %copy-start.6 = (f32[8]{0:T(128)S(1)}, f32[8]{0:T(128)}, u32[]{:S(2)}) copy-start(f32[8]{0:T(128)} %get-tuple-element.43) | copy-start | bytes 100
  92.0 7.1 %copy-start.7 = (f32[8]{0:T(128)S(1)}, f32[8]{0:T(128)}, u32[]{:S(2)}) copy-start(f32[8]{0:T(128)} %get-tuple-element.44) | copy-start | bytes 100
  92.0 7.1 %copy-start.9 = (f32[8]{0:T(128)S(1)}, f32[8]{0:T(128)}, u32[]{:S(2)}) copy-start(f32[8]{0:T(128)} %param.10) | copy-start | bytes 100
  94.5 51.0 %all-to-all-start.2 = ((f32[4,128,128]{1,2,0:T(8,128)}), f32[4,128,128]{1,2,0:T(8,128)S(1)}, u32[]{:S(2)}, u32[]{:S(2)}) async-start(f32[4,128,128]{1,2,0:T(8,128)} %maximum_multiply_fusion), calls=%async_computation.2 | async-start | bytes 524288 | tf_op jit(solution)/shard_map/all_to_all | solution.py:25

commit v2 on v1

v2 whole, which is shorter than its diff:
```python
import functools
import math

import jax
import jax.numpy as jnp
from jax import lax
from jax.experimental import pallas as pl
from jax.experimental.pallas import tpu as pltpu
from jax.sharding import Mesh
from jax.sharding import PartitionSpec as P


F32 = jnp.float32
BF16 = jnp.bfloat16
GRP = ("yh", "core")
ROW = ("yl", "zh", "zl")
QUAD = ("yl", "zl")
LANES = 128
WHOLE = pl.BlockSpec(memory_space=pltpu.VMEM)
SCALARS = pl.BlockSpec(memory_space=pltpu.SMEM)


def call(kernel, **given):
    def run(*args):
        return pl.pallas_call(kernel, **given)(*args)

    return run


def chain(n):
    return [(i, i + 1) for i in range(n - 1)]


def back(n):
    return [(i + 1, i) for i in range(n - 1)]


def exchanged(value, axes):
    return lax.all_to_all(value, axes, 0, 0, tiled=True)


def shape(dims, kind):
    return jax.ShapeDtypeStruct(dims, kind)


def dot_t(a, b):
    return lax.dot_general(a, b, (((0,), (0,)), ((), ())), preferred_element_type=F32)


def dot(a, b):
    return lax.dot_general(a, b, (((1,), (0,)), ((), ())), preferred_element_type=F32)


GRANT = pltpu.CompilerParams(vmem_limit_bytes=16 * 2**20)


def cost(flops):
    return pl.CostEstimate(flops=flops, bytes_accessed=1 << 20, transcendentals=0)


def faces_kernel(u_ref, low_ref, x_first, x_last, y_first, y_last):
    u = u_ref[0]
    low = u.astype(BF16)
    low_ref[0] = low
    x_first[0] = u[:1]
    x_last[0] = u[-1:]
    y_first[0] = low[:, :LANES]
    y_last[0] = low[:, -LANES:]


def faces(u):
    species, wx, wy = u.shape
    plane = pl.BlockSpec((1, wx, wy), lambda s: (s, 0, 0))
    line = pl.BlockSpec((1, 1, wy), lambda s: (s, 0, 0))
    strip = pl.BlockSpec((1, wx, LANES), lambda s: (s, 0, 0))
    return call(
        faces_kernel,
        grid=(species,),
        in_specs=[plane],
        out_specs=[plane, line, line, strip, strip],
        out_shape=[
            shape(u.shape, BF16),
            shape((species, 1, wy), F32),
            shape((species, 1, wy), F32),
            shape((species, wx, LANES), BF16),
            shape((species, wx, LANES), BF16),
        ],
        cost_estimate=cost(10**8),
        compiler_params=GRANT,
    )(u)


def stencil_kernel(rates, speeds, u_ref, zp, zn, xp, xn, yp, yn, kappa, out):
    s = pl.program_id(0)
    u = u_ref[0]
    wx, wy = u.shape
    rows = lax.broadcasted_iota(jnp.int32, u.shape, 0)
    lanes = lax.broadcasted_iota(jnp.int32, u.shape, 1)
    z_prev, z_next = zp[0].astype(F32), zn[0].astype(F32)
    x_prev = jnp.where(rows == 0, xp[0], pltpu.roll(u, 1, 0))
    x_next = jnp.where(rows == wx - 1, xn[0], pltpu.roll(u, wx - 1, 0))
    y_prev = jnp.where(lanes == 0, yp[0].astype(F32)[:, -1:], pltpu.roll(u, 1, 1))
    y_next = jnp.where(lanes == wy - 1, yn[0].astype(F32)[:, :1], pltpu.roll(u, wy - 1, 1))
    laplace = z_next + z_prev + x_next + x_prev + y_next + y_prev - 6.0 * u
    transport = (
        speeds[s, 0] * (z_next - z_prev)
        + speeds[s, 1] * (x_next - x_prev)
        + speeds[s, 2] * (y_next - y_prev)
    )
    out[0] = u + kappa[...] * rates[s] * laplace - 0.5 * transport


def stencil(u, kappa, rates, speeds):
    species, wx, wy = u.shape
    n_grp, n_row, n_col = lax.axis_size(GRP), lax.axis_size(ROW), lax.axis_size("x")
    low, x_first, x_last, y_first, y_last = faces(u)
    z_prev = lax.ppermute(low, GRP, chain(n_grp))
    z_next = lax.ppermute(low, GRP, back(n_grp))
    x_prev = lax.ppermute(x_last, ROW, chain(n_row))
    x_next = lax.ppermute(x_first, ROW, back(n_row))
    y_prev = lax.ppermute(y_last, "x", chain(n_col))
    y_next = lax.ppermute(y_first, "x", back(n_col))
    plane = pl.BlockSpec((1, wx, wy), lambda s: (s, 0, 0))
    line = pl.BlockSpec((1, 1, wy), lambda s: (s, 0, 0))
    strip = pl.BlockSpec((1, wx, LANES), lambda s: (s, 0, 0))
    return call(
        stencil_kernel,
        grid=(species,),
        in_specs=[SCALARS, SCALARS, plane, plane, plane, line, line, strip, strip]
        + [pl.BlockSpec((wx, wy), lambda s: (0, 0))],
        out_specs=plane,
        out_shape=shape(u.shape, F32),
        cost_estimate=cost(10**9),
        compiler_params=GRANT,
    )(rates, speeds, u, z_prev, z_next, x_prev, x_next, y_prev, y_next, kappa)


def project_kernel(lines, basis, out):
    quad, own, wx, wy = lines.shape
    rank = basis.shape[-1]
    b = basis[...].reshape(quad * wx, rank)
    for s in range(own):
        block = lines[:, s].reshape(quad * wx, wy)
        out[s] = dot_t(block, b)


def round_kernel(parts, out):
    total = parts[0]
    for k in range(1, parts.shape[0]):
        total = total + parts[k]
    low = total.astype(BF16)
    for k in range(out.shape[0]):
        out[k] = low


def moments_kernel(scale, lines, projected, basis, out):
    quad, own, wx, wy = lines.shape
    rank = projected.shape[-1]
    columns, part = out.shape[0], wx // out.shape[0]
    for s in range(own):
        core = dot_t(projected[s], basis[...])
        high = core.astype(BF16)
        low = (core - high.astype(F32)).astype(BF16)
        for k in range(columns):
            out[k, pl.ds(s * rank, rank)] = high
            out[k, pl.ds((own + s) * rank, rank)] = low
    total = dot(lines[:, 0].reshape(quad * wx, wy), projected[0])
    for s in range(1, own):
        total = total + dot(lines[:, s].reshape(quad * wx, wy), projected[s])
    total = (scale * total).astype(BF16)
    first = 2 * own * rank
    for q in range(quad):
        for k in range(columns):
            rows = total[q * wx + k * part : q * wx + (k + 1) * part]
            out[k, pl.ds(first + q * part, part)] = rows


def mix_kernel(scale, zh, parts, projected, out):
    own, wy, rank = projected.shape
    columns, quad = parts.shape[0], out.shape[0]
    part = (parts.shape[1] - 2 * own * rank) // quad
    half_rows = 2 * (out.shape[1] - own * rank - part)
    totals = [0.0, 0.0]
    for s in range(own):
        total = 0.0
        for first in (s * rank, (own + s) * rank):
            for k in range(columns):
                total = total + parts[k, pl.ds(first, rank)].astype(F32)
        low = total.astype(BF16)
        for q in range(quad):
            out[q, pl.ds(s * rank, rank)] = low
        for h in range(2):
            first = pl.multiple_of(h * (wy // 2) + zh[0] * half_rows, half_rows)
            totals[h] = totals[h] + dot(projected[s, pl.ds(first, half_rows), :], low)
    for q in range(quad):
        total = 0.0
        for k in range(columns):
            total = total + parts[k, pl.ds(2 * own * rank + q * part, part)].astype(F32)
        out[q, pl.ds(own * rank, part)] = total.astype(BF16)
    for h in range(2):
        rows = (scale * totals[h]).astype(BF16)
        for low in range(2):
            size = half_rows // 2
            out[2 * h + low, pl.ds(own * rank + part, size)] = rows[low * size : (low + 1) * size]


def spread_kernel(parts, core, out):
    quad, n = parts.shape[0], core.shape[1]
    total = 0.0
    for q in range(quad):
        core[q] = parts[q, :n].astype(F32)
        total = total + parts[q, n:].astype(F32)
    low = total.astype(BF16)
    for k in range(out.shape[0]):
        out[k] = low


def last_kernel(column, parts, gram_x, gram_y):
    groups, columns = parts.shape[:2]
    part = gram_x.shape[0] // columns
    for c in range(columns):
        total = parts[0, c, :part].astype(F32)
        for g in range(1, groups):
            total = total + parts[g, c, :part].astype(F32)
        gram_x[pl.ds(c * part, part)] = total
    mine = column[0]
    total = parts[0, mine, part:].astype(F32)
    for g in range(1, groups):
        total = total + parts[g, mine, part:].astype(F32)
    gram_y[...] = total


def on_device(field, previous, kappa, rates, speeds, basis_x, basis_y):
    species, depth, width_x, width_y = field.shape
    rank = basis_x.shape[1]
    n_quad, n_zh, n_col = lax.axis_size(QUAD), lax.axis_size("zh"), lax.axis_size("x")
    n_grp, n_row = lax.axis_size(GRP), lax.axis_size(ROW)
    own = species // n_quad
    grid_x, grid_y, grid_z = width_x * n_row, width_y * n_col, depth * n_grp
    part_y = width_y // n_row
    scale_x = math.sqrt(grid_x) / (species * grid_z * grid_y)
    scale_y = math.sqrt(grid_y) / (species * grid_z * rank)
    zh = lax.axis_index("zh")

    lines = exchanged(previous.reshape(n_quad, own, width_x, width_y), QUAD)
    bx = basis_x.reshape(lax.axis_size("yl"), n_zh, lax.axis_size("zl"), width_x, rank)
    bx = lax.dynamic_index_in_dim(bx, zh, 1, keepdims=False).reshape(n_quad, width_x, rank)
    by = lax.dynamic_slice_in_dim(basis_y, lax.axis_index("x") * width_y, width_y, 0)
    advanced = stencil(field[:, 0], kappa[0], rates, speeds)[:, None]

    partial = call(
        project_kernel,
        in_specs=[WHOLE, WHOLE],
        out_specs=WHOLE,
        out_shape=shape((own, width_y, rank), F32),
        cost_estimate=cost(2 * n_quad * width_x * own * width_y * rank),
        compiler_params=GRANT,
    )(lines, bx)
    piece = own * width_y // n_zh
    arrived = exchanged(partial.reshape(n_zh, piece, rank), "zh")
    mine = call(
        round_kernel,
        in_specs=[WHOLE],
        out_specs=WHOLE,
        out_shape=shape((n_zh, piece, rank), BF16),
        cost_estimate=cost(10**7),
        compiler_params=GRANT,
    )(arrived)
    projected = exchanged(mine, "zh").reshape(own, width_y, rank)

    part_x = width_x // n_col
    moments = call(
        functools.partial(moments_kernel, scale_x),
        in_specs=[WHOLE, WHOLE, WHOLE],
        out_specs=WHOLE,
        out_shape=shape((n_col, 2 * own * rank + n_quad * part_x, rank), BF16),
        cost_estimate=cost(4 * n_quad * width_x * own * width_y * rank),
        compiler_params=GRANT,
    )(lines, projected, by)
    mixed = call(
        functools.partial(mix_kernel, scale_y),
        in_specs=[SCALARS, WHOLE, WHOLE],
        out_specs=WHOLE,
        out_shape=shape((n_quad, own * rank + part_x + part_y, rank), BF16),
        cost_estimate=cost(10**8),
        compiler_params=GRANT,
    )(zh.reshape(1), exchanged(moments, "x"), projected)
    core, rows = call(
        spread_kernel,
        in_specs=[WHOLE],
        out_specs=[WHOLE, WHOLE],
        out_shape=[
            shape((n_quad, own * rank, rank), F32),
            shape((n_grp * n_col, part_x + part_y, rank), BF16),
        ],
        cost_estimate=cost(10**8),
        compiler_params=GRANT,
    )(exchanged(mixed, QUAD))
    core = core.reshape(species, 1, rank, rank)
    rows = exchanged(rows, GRP + ("x",))
    gram_x, gram_y = call(
        last_kernel,
        in_specs=[SCALARS, WHOLE],
        out_specs=[WHOLE, WHOLE],
        out_shape=[shape((width_x, rank), F32), shape((part_y, rank), F32)],
        cost_estimate=cost(10**7),
        compiler_params=GRANT,
    )(lax.axis_index("x").reshape(1), rows.reshape(n_grp, n_col, part_x + part_y, rank))
    return (advanced, core, gram_x, gram_y)


def solution(mesh):
    split = Mesh(
        mesh.devices.reshape(4, 2, 2, 6, 2, 4), ("yh", "core", "yl", "zh", "zl", "x")
    )
    block = P(None, GRP, ROW, "x")
    return jax.shard_map(
        on_device,
        mesh=split,
        in_specs=(block, block, P(GRP, ROW, "x"), P(), P(), P(), P()),
        out_specs=(block, P(None, GRP, None, None), P(ROW, None), P(("x", *ROW), None)),
        check_vma=False,
    )
```

time: 178 us -> 139 us (0.78)
  the two profiles are of different devices: /device:TPU:57 before, /device:TPU:42 now
where the time goes in v2:
time: 139 us; the launch traced here: 138 us
  blocking collectives  44.4 us (32%)
  starting transfers between devices  43.3 us (31%)
  waiting for transfers between devices  29.8 us (21%)
  Pallas kernels  12.9 us (9%)
  local copies, waits for them, and re-layouts  6.61 us (5%)
    all_to_all x2, blocking collectives, exchanged(): return lax.all_to_all(value, axes, 0, 0, tiled=True)  44.4 us
    all_to_all x4, starting transfers between devices, exchanged(): return lax.all_to_all(value, axes, 0, 0, tiled=True)  23.8 us
    all_to_all x4, waiting for transfers between devices, exchanged(): return lax.all_to_all(value, axes, 0, 0, tiled=True)  22.1 us
    pallas_call x8, Pallas kernels, run(): return pl.pallas_call(kernel, **given)(*args)  12.9 us
    ppermute x1, starting transfers between devices, stencil(): z_next = lax.ppermute(low, GRP, back(n_grp))  5.75 us
    unnamed x19, local copies, waits for them, and re-layouts  5.71 us
    ppermute x1, waiting for transfers between devices, stencil(): x_prev = lax.ppermute(x_last, ROW, chain(n_row))  4.53 us
    ppermute x1, starting transfers between devices, stencil(): x_prev = lax.ppermute(x_last, ROW, chain(n_row))  3.37 us
  transfers between devices with their start and end apart: 10, of which 4 were waited for; matrix products, arithmetic and copies ran while one was open for 1% of the time, Pallas kernels for 7%

profile of v2, /device:TPU:42, one launch (start us, length us, event | category | flops | bytes accessed | tf_op | source)
XLA Modules:
  0.0 137.8 jit_solution(9130045870623045520)
XLA Ops:
  0.6 5.2 %all-to-all-start = ((bf16[4,2,128,384]{3,2,1,0:T(8,128)(2,1)}), bf16[4,2,128,384]{3,2,1,0:T(8,128)(2,1)S(1)}, u32[]{:S(2)}, u32[]{:S(2)}) async-start(bf16[4,2,128,384]{3,2,1,0:T(8,128)(2,1)} %bitcast.28), calls=%async_computation | async-start | bytes 1572864 | tf_op jit(solution)/shard_map/all_to_all | solution.py:39
  5.9 10.2 %all-to-all-done.lines = bf16[4,2,128,384]{3,2,1,0:T(8,128)(2,1)S(1)} async-done(((bf16[4,2,128,384]{3,2,1,0:T(8,128)(2,1)}), bf16[4,2,128,384]{3,2,1,0:T(8,128)(2,1)S(1)}, u32[]{:S(2)}, u32[]{:S(2)}) %all-to-all-start) | async-done | bytes 786464 | tf_op jit(solution)/shard_map/all_to_all | solution.py:39
  16.6 32.3 %all_to_all.30.parts = f32[6,128,128]{2,1,0:T(8,128)S(1)} all-to-all(f32[6,128,128]{2,1,0:T(8,128)S(1)} %bitcast.24), channel_id=1, replica_groups=mesh['yh'=4,'core'=2,'yl'=2,'zh'=6,'zl'=2,'x'=4] {'zh'}, dimensions={0} | all-to-all | bytes 786432 | tf_op jit(solution)/shard_map/all_to_all | solution.py:39
  48.8 0.7 shard_map.105
  49.5 4.4 %all-to-all-start.2 = ((bf16[6,128,128]{2,1,0:T(8,128)(2,1)}), bf16[6,128,128]{2,1,0:T(8,128)(2,1)S(1)}, u32[]{:S(2)}, u32[]{:S(2)}) async-start(bf16[6,128,128]{2,1,0:T(8,128)(2,1)} %shard_map.105), calls=%async_computation.2 | async-start | bytes 393216 | tf_op jit(solution)/shard_map/all_to_all | solution.py:39
  53.9 0.9 constant_dynamic-slice_fusion.basis
  54.8 11.8 %all-to-all-done.2 = bf16[6,128,128]{2,1,0:T(8,128)(2,1)S(1)} async-done(((bf16[6,128,128]{2,1,0:T(8,128)(2,1)}), bf16[6,128,128]{2,1,0:T(8,128)(2,1)S(1)}, u32[]{:S(2)}, u32[]{:S(2)}) %all-to-all-start.2) | async-done | bytes 196640 | tf_op jit(solution)/shard_map/all_to_all | solution.py:39
  66.6 0.5 shard_map.106
  67.1 12.1 %all_to_all.31.parts = bf16[4,640,128]{2,1,0:T(8,128)(2,1)S(1)} all-to-all(bf16[4,640,128]{2,1,0:T(8,128)(2,1)S(1)} %shard_map.106), channel_id=1, replica_groups=mesh['yh'=4,'core'=2,'yl'=2,'zh'=6,'zl'=2,'x'=4] {'x'}, dimensions={0} | all-to-all | bytes 1310720 | tf_op jit(solution)/shard_map/all_to_all | solution.py:39
  79.2 0.9 shard_map.107
  80.1 5.3 %all-to-all-start.4 = ((bf16[4,304,128]{2,1,0:T(8,128)(2,1)}), bf16[4,304,128]{2,1,0:T(8,128)(2,1)S(1)}, u32[]{:S(2)}, u32[]{:S(2)}) async-start(bf16[4,304,128]{2,1,0:T(8,128)(2,1)} %shard_map.107), calls=%async_computation.4 | async-start | bytes 622592 | tf_op jit(solution)/shard_map/all_to_all | solution.py:39
  85.4 2.7 %shard_map.102 = (bf16[8,128,384]{2,1,0:T(8,128)(2,1)}, f32[8,1,384]{2,1,0:T(1,128)S(1)}, f32[8,1,384]{2,1,0:T(1,128)S(1)}, bf16[8,128,128]{2,1,0:T(8,128)(2,1)S(1)}, bf16[8,128,128]{2,1,0:T(8,128)(2,1)S(1)}) custom-call(f32[8,128,384]{2,1,0:T(8,128)S(1)} %bitcast.19), custom_call_target="tpu_custom_call" | custom-call | flops 100000000 | bytes 1048576 | tf_op jit(solution)/shard_map/pallas_call | solution.py:25
  88.1 0.7 copy-done.5
  88.8 0.7 copy-done.6
  89.5 0.6 copy-done.7
  90.1 0.6 copy-done.8
  90.7 1.9 %collective-permute-start = (bf16[8,128,384]{2,1,0:T(8,128)(2,1)}, bf16[8,128,384]{2,1,0:T(8,128)(2,1)S(1)}, u32[]{:S(2)}, u32[]{:S(2)}) collective-permute-start(bf16[8,128,384]{2,1,0:T(8,128)(2,1)} %get-tuple-element.13), channel_id=1, source_target_pairs={{0,96},{96,192},{192,288},{288,384},{384,480},{480,576},{576,672},... | collective-permute-start | bytes 2359304 | tf_op jit(solution)/shard_map/ppermute | solution.py:117
  92.6 5.8 %collective-permute-start.1 = (bf16[8,128,384]{2,1,0:T(8,128)(2,1)}, bf16[8,128,384]{2,1,0:T(8,128)(2,1)}, u32[]{:S(2)}, u32[]{:S(2)}) collective-permute-start(bf16[8,128,384]{2,1,0:T(8,128)(2,1)} %get-tuple-element.13), channel_id=1, source_target_pairs={{96,0},{192,96},{288,192},{384,288},{480,384},{576,480},{672,576},... | collective-permute-start | bytes 2359304 | tf_op jit(solution)/shard_map/ppermute | solution.py:118
  98.3 0.8 shard_map.108
  99.2 0.8 copy-done.2
  99.9 8.9 %all-to-all-start.5 = ((bf16[32,48,128]{2,1,0:T(8,128)(2,1)}), bf16[32,48,128]{2,1,0:T(8,128)(2,1)S(1)}, u32[]{:S(2)}, u32[]{:S(2)}) async-start(bf16[32,48,128]{2,1,0:T(8,128)(2,1)} %copy-done.2), calls=%async_computation.5 | async-start | bytes 786432 | tf_op jit(solution)/shard_map/all_to_all | solution.py:39
  108.8 3.4 %collective-permute-start.4 = (bf16[8,128,128]{2,1,0:T(8,128)(2,1)}, bf16[8,128,128]{2,1,0:T(8,128)(2,1)}, u32[]{:S(2)}, u32[]{:S(2)}) collective-permute-start(bf16[8,128,128]{2,1,0:T(8,128)(2,1)} %copy-done.6), channel_id=1, source_target_pairs={{0,1},{1,2},{2,3},{4,5},{5,6},{6,7},{8,9},{9,10},{10,11},{12,13},{... | collective-permute-start | bytes 786440 | tf_op jit(solution)/shard_map/ppermute | solution.py:121
  112.2 3.2 %collective-permute-start.5 = (bf16[8,128,128]{2,1,0:T(8,128)(2,1)}, bf16[8,128,128]{2,1,0:T(8,128)(2,1)}, u32[]{:S(2)}, u32[]{:S(2)}) collective-permute-start(bf16[8,128,128]{2,1,0:T(8,128)(2,1)} %copy-done.5), channel_id=1, source_target_pairs={{1,0},{2,1},{3,2},{5,4},{6,5},{7,6},{9,8},{10,9},{11,10},{13,12},{... | collective-permute-start | bytes 786440 | tf_op jit(solution)/shard_map/ppermute | solution.py:122
  115.4 3.4 %collective-permute-start.2 = (f32[8,1,384]{2,1,0:T(1,128)}, f32[8,1,384]{2,1,0:T(1,128)S(1)}, u32[]{:S(2)}, u32[]{:S(2)}) collective-permute-start(f32[8,1,384]{2,1,0:T(1,128)} %copy-done.8), channel_id=1, source_target_pairs={{0,4},{4,8},{8,12},{12,16},{16,20},{20,24},{24,28},{28,32},{32,36}... | collective-permute-start | bytes 36872 | tf_op jit(solution)/shard_map/ppermute | solution.py:119
  118.8 4.5 %collective-permute-done.2.xp = f32[8,1,384]{2,1,0:T(1,128)S(1)} collective-permute-done((f32[8,1,384]{2,1,0:T(1,128)}, f32[8,1,384]{2,1,0:T(1,128)S(1)}, u32[]{:S(2)}, u32[]{:S(2)}) %collective-permute-start.2) | collective-permute-done | bytes 12320 | tf_op jit(solution)/shard_map/ppermute | solution.py:119
  123.3 1.9 %collective-permute-start.3 = (f32[8,1,384]{2,1,0:T(1,128)}, f32[8,1,384]{2,1,0:T(1,128)}, u32[]{:S(2)}, u32[]{:S(2)}) collective-permute-start(f32[8,1,384]{2,1,0:T(1,128)} %copy-done.7), channel_id=1, source_target_pairs={{4,0},{8,4},{12,8},{16,12},{20,16},{24,20},{28,24},{32,28},{36,32}... | collective-permute-start | bytes 36872 | tf_op jit(solution)/shard_map/ppermute | solution.py:120
  125.2 0.8 copy.11.speeds
  126.0 3.2 %collective-permute-done.3.xn = f32[8,1,384]{2,1,0:T(1,128)} collective-permute-done((f32[8,1,384]{2,1,0:T(1,128)}, f32[8,1,384]{2,1,0:T(1,128)}, u32[]{:S(2)}, u32[]{:S(2)}) %collective-permute-start.3) | collective-permute-done | bytes 12320 | tf_op jit(solution)/shard_map/ppermute | solution.py:120
  129.2 0.9 copy-done.3
  130.2 0.7 copy-done.4
  130.8 6.3 %shard_map.103 = f32[8,128,384]{2,1,0:T(8,128)} custom-call(f32[8]{0:T(128)S(1)} %copy-done.4, f32[8,3]{1,0:T(8,128)S(1)} %copy.11.speeds, f32[8,128,384]{2,1,0:T(8,128)S(1)} %bitcast.20, bf16[8,128,384]{2,1,0:T(8,128)(2,1)S(1)} %collective-permute-done.zp, bf16[8,128,384]{2,1,0:T(8,128)(2,1)} %collective-permute-done.1.zn, ...), custom_call_target="tpu_custom_call" | custom-call | flops 1000000000 | bytes 1048576 | tf_op jit(solution)/shard_map/pallas_call | solution.py:25
  137.1 0.7 shard_map.109
  (19 shorter events, 0.5 us)
Async XLA Ops:
  0.6 5.3 %copy-start = (bf16[3072,128]{1,0:T(8,128)(2,1)S(1)}, bf16[3072,128]{1,0:T(8,128)(2,1)}, u32[]{:S(2)}) copy-start(bf16[3072,128]{1,0:T(8,128)(2,1)} %param.12) | copy-start | bytes 2359300
  0.6 15.5 %all-to-all-start = ((bf16[4,2,128,384]{3,2,1,0:T(8,128)(2,1)}), bf16[4,2,128,384]{3,2,1,0:T(8,128)(2,1)S(1)}, u32[]{:S(2)}, u32[]{:S(2)}) async-start(bf16[4,2,128,384]{3,2,1,0:T(8,128)(2,1)} %bitcast.28), calls=%async_computation | async-start | bytes 1572864 | tf_op jit(solution)/shard_map/all_to_all | solution.py:39
  49.5 17.1 %all-to-all-start.2 = ((bf16[6,128,128]{2,1,0:T(8,128)(2,1)}), bf16[6,128,128]{2,1,0:T(8,128)(2,1)S(1)}, u32[]{:S(2)}, u32[]{:S(2)}) async-start(bf16[6,128,128]{2,1,0:T(8,128)(2,1)} %shard_map.105), calls=%async_computation.2 | async-start | bytes 393216 | tf_op jit(solution)/shard_map/all_to_all | solution.py:39
  67.1 18.3 %copy-start.1 = (f32[8,1,128,384]{3,2,1,0:T(8,128)S(1)}, f32[8,1,128,384]{3,2,1,0:T(8,128)}, u32[]{:S(2)}) copy-start(f32[8,1,128,384]{3,2,1,0:T(8,128)} %param.7) | copy-start | bytes 4718596
  80.1 18.2 %all-to-all-start.4 = ((bf16[4,304,128]{2,1,0:T(8,128)(2,1)}), bf16[4,304,128]{2,1,0:T(8,128)(2,1)S(1)}, u32[]{:S(2)}, u32[]{:S(2)}) async-start(bf16[4,304,128]{2,1,0:T(8,128)(2,1)} %shard_map.107), calls=%async_computation.4 | async-start | bytes 622592 | tf_op jit(solution)/shard_map/all_to_all | solution.py:39
  88.1 0.7 copy-start.5
  88.8 0.7 copy-start.6
  89.5 0.6 copy-start.7
  90.1 0.6 copy-start.8
  90.7 38.6 %collective-permute-start = (bf16[8,128,384]{2,1,0:T(8,128)(2,1)}, bf16[8,128,384]{2,1,0:T(8,128)(2,1)S(1)}, u32[]{:S(2)}, u32[]{:S(2)}) collective-permute-start(bf16[8,128,384]{2,1,0:T(8,128)(2,1)} %get-tuple-element.13), channel_id=1, source_target_pairs={{0,96},{96,192},{192,288},{288,384},{384,480},{480,576},{576,672},... | collective-permute-start | bytes 2359304 | tf_op jit(solution)/shard_map/ppermute | solution.py:117
  92.6 36.6 %collective-permute-start.1 = (bf16[8,128,384]{2,1,0:T(8,128)(2,1)}, bf16[8,128,384]{2,1,0:T(8,128)(2,1)}, u32[]{:S(2)}, u32[]{:S(2)}) collective-permute-start(bf16[8,128,384]{2,1,0:T(8,128)(2,1)} %get-tuple-element.13), channel_id=1, source_target_pairs={{96,0},{192,96},{288,192},{384,288},{480,384},{576,480},{672,576},... | collective-permute-start | bytes 2359304 | tf_op jit(solution)/shard_map/ppermute | solution.py:118
  99.2 0.8 copy-start.2
  99.9 37.2 %all-to-all-start.5 = ((bf16[32,48,128]{2,1,0:T(8,128)(2,1)}), bf16[32,48,128]{2,1,0:T(8,128)(2,1)S(1)}, u32[]{:S(2)}, u32[]{:S(2)}) async-start(bf16[32,48,128]{2,1,0:T(8,128)(2,1)} %copy-done.2), calls=%async_computation.5 | async-start | bytes 786432 | tf_op jit(solution)/shard_map/all_to_all | solution.py:39
  108.8 20.4 %collective-permute-start.4 = (bf16[8,128,128]{2,1,0:T(8,128)(2,1)}, bf16[8,128,128]{2,1,0:T(8,128)(2,1)}, u32[]{:S(2)}, u32[]{:S(2)}) collective-permute-start(bf16[8,128,128]{2,1,0:T(8,128)(2,1)} %copy-done.6), channel_id=1, source_target_pairs={{0,1},{1,2},{2,3},{4,5},{5,6},{6,7},{8,9},{9,10},{10,11},{12,13},{... | collective-permute-start | bytes 786440 | tf_op jit(solution)/shard_map/ppermute | solution.py:121
  112.2 17.0 %collective-permute-start.5 = (bf16[8,128,128]{2,1,0:T(8,128)(2,1)}, bf16[8,128,128]{2,1,0:T(8,128)(2,1)}, u32[]{:S(2)}, u32[]{:S(2)}) collective-permute-start(bf16[8,128,128]{2,1,0:T(8,128)(2,1)} %copy-done.5), channel_id=1, source_target_pairs={{1,0},{2,1},{3,2},{5,4},{6,5},{7,6},{9,8},{10,9},{11,10},{13,12},{... | collective-permute-start | bytes 786440 | tf_op jit(solution)/shard_map/ppermute | solution.py:122
  115.4 7.9 %collective-permute-start.2 = (f32[8,1,384]{2,1,0:T(1,128)}, f32[8,1,384]{2,1,0:T(1,128)S(1)}, u32[]{:S(2)}, u32[]{:S(2)}) collective-permute-start(f32[8,1,384]{2,1,0:T(1,128)} %copy-done.8), channel_id=1, source_target_pairs={{0,4},{4,8},{8,12},{12,16},{16,20},{20,24},{24,28},{28,32},{32,36}... | collective-permute-start | bytes 36872 | tf_op jit(solution)/shard_map/ppermute | solution.py:119
  123.3 5.9 %collective-permute-start.3 = (f32[8,1,384]{2,1,0:T(1,128)}, f32[8,1,384]{2,1,0:T(1,128)}, u32[]{:S(2)}, u32[]{:S(2)}) collective-permute-start(f32[8,1,384]{2,1,0:T(1,128)} %copy-done.7), channel_id=1, source_target_pairs={{4,0},{8,4},{12,8},{16,12},{20,16},{24,20},{28,24},{32,28},{36,32}... | collective-permute-start | bytes 36872 | tf_op jit(solution)/shard_map/ppermute | solution.py:120
  129.2 0.9 copy-start.3
  130.1 0.7 copy-start.4

commit v3 on v2

--- a/solution.py
+++ b/solution.py
@@ -37,6 +37,10 @@
 
 def exchanged(value, axes):
     return lax.all_to_all(value, axes, 0, 0, tiled=True)
+
+
+def stored(dims, kind):
+    return pltpu.HBM(dims, kind)
 
 
 def shape(dims, kind):
@@ -79,11 +83,11 @@
         in_specs=[plane],
         out_specs=[plane, line, line, strip, strip],
         out_shape=[
-            shape(u.shape, BF16),
-            shape((species, 1, wy), F32),
-            shape((species, 1, wy), F32),
-            shape((species, wx, LANES), BF16),
-            shape((species, wx, LANES), BF16),
+            stored(u.shape, BF16),
+            stored((species, 1, wy), F32),
+            stored((species, 1, wy), F32),
+            stored((species, wx, LANES), BF16),
+            stored((species, wx, LANES), BF16),
         ],
         cost_estimate=cost(10**8),
         compiler_params=GRANT,
@@ -156,7 +160,7 @@
 def moments_kernel(scale, lines, projected, basis, out):
     quad, own, wx, wy = lines.shape
     rank = projected.shape[-1]
-    columns, part = out.shape[0], wx // out.shape[0]
+    columns = out.shape[0]
     for s in range(own):
         core = dot_t(projected[s], basis[...])
         high = core.astype(BF16)
@@ -168,11 +172,8 @@
     for s in range(1, own):
         total = total + dot(lines[:, s].reshape(quad * wx, wy), projected[s])
     total = (scale * total).astype(BF16)
-    first = 2 * own * rank
-    for q in range(quad):
-        for k in range(columns):
-            rows = total[q * wx + k * part : q * wx + (k + 1) * part]
-            out[k, pl.ds(first + q * part, part)] = rows
+    for k in range(columns):
+        out[k, pl.ds(2 * own * rank, quad * wx)] = total
 
 
 def mix_kernel(scale, zh, parts, projected, out):
@@ -215,19 +216,13 @@
         out[k] = low
 
 
-def last_kernel(column, parts, gram_x, gram_y):
-    groups, columns = parts.shape[:2]
-    part = gram_x.shape[0] // columns
-    for c in range(columns):
-        total = parts[0, c, :part].astype(F32)
-        for g in range(1, groups):
-            total = total + parts[g, c, :part].astype(F32)
-        gram_x[pl.ds(c * part, part)] = total
-    mine = column[0]
-    total = parts[0, mine, part:].astype(F32)
-    for g in range(1, groups):
-        total = total + parts[g, mine, part:].astype(F32)
-    gram_y[...] = total
+def last_kernel(parts, gram_x, gram_y):
+    total = parts[0].astype(F32)
+    for g in range(1, parts.shape[0]):
+        total = total + parts[g].astype(F32)
+    n = gram_x.shape[0]
+    gram_x[...] = total[:n]
+    gram_y[...] = total[n:]
 
 
 def on_device(field, previous, kappa, rates, speeds, basis_x, basis_y):
@@ -252,7 +247,7 @@
         project_kernel,
         in_specs=[WHOLE, WHOLE],
         out_specs=WHOLE,
-        out_shape=shape((own, width_y, rank), F32),
+        out_shape=stored((own, width_y, rank), F32),
         cost_estimate=cost(2 * n_quad * width_x * own * width_y * rank),
         compiler_params=GRANT,
     )(lines, bx)
@@ -262,18 +257,17 @@
         round_kernel,
         in_specs=[WHOLE],
         out_specs=WHOLE,
-        out_shape=shape((n_zh, piece, rank), BF16),
+        out_shape=stored((n_zh, piece, rank), BF16),
         cost_estimate=cost(10**7),
         compiler_params=GRANT,
     )(arrived)
     projected = exchanged(mine, "zh").reshape(own, width_y, rank)
 
-    part_x = width_x // n_col
     moments = call(
         functools.partial(moments_kernel, scale_x),
         in_specs=[WHOLE, WHOLE, WHOLE],
         out_specs=WHOLE,
-        out_shape=shape((n_col, 2 * own * rank + n_quad * part_x, rank), BF16),
+        out_shape=shape((n_col, 2 * own * rank + n_quad * width_x, rank), BF16),
         cost_estimate=cost(4 * n_quad * width_x * own * width_y * rank),
         compiler_params=GRANT,
     )(lines, projected, by)
@@ -281,7 +275,7 @@
         functools.partial(mix_kernel, scale_y),
         in_specs=[SCALARS, WHOLE, WHOLE],
         out_specs=WHOLE,
-        out_shape=shape((n_quad, own * rank + part_x + part_y, rank), BF16),
+        out_shape=shape((n_quad, own * rank + width_x + part_y, rank), BF16),
         cost_estimate=cost(10**8),
         compiler_params=GRANT,
     )(zh.reshape(1), exchanged(moments, "x"), projected)
@@ -291,21 +285,20 @@
         out_specs=[WHOLE, WHOLE],
         out_shape=[
             shape((n_quad, own * rank, rank), F32),
-            shape((n_grp * n_col, part_x + part_y, rank), BF16),
+            stored((n_grp, width_x + part_y, rank), BF16),
         ],
         cost_estimate=cost(10**8),
         compiler_params=GRANT,
     )(exchanged(mixed, QUAD))
     core = core.reshape(species, 1, rank, rank)
-    rows = exchanged(rows, GRP + ("x",))
     gram_x, gram_y = call(
         last_kernel,
-        in_specs=[SCALARS, WHOLE],
+        in_specs=[WHOLE],
         out_specs=[WHOLE, WHOLE],
         out_shape=[shape((width_x, rank), F32), shape((part_y, rank), F32)],
         cost_estimate=cost(10**7),
         compiler_params=GRANT,
-    )(lax.axis_index("x").reshape(1), rows.reshape(n_grp, n_col, part_x + part_y, rank))
+    )(exchanged(rows, GRP))
     return (advanced, core, gram_x, gram_y)
 
 

time: 139 us -> 138 us (level)
  local copies, waits for them, and re-layouts: 6.61 us -> 3.26 us
  blocking collectives: 44.4 us -> 47.3 us
    unnamed x19 -> x9, local copies, waits for them, and re-layouts: 5.71 us -> 2.35 us
    all_to_all x2, blocking collectives: 44.4 us -> 47.3 us  [exchanged(): return lax.all_to_all(value, axes, 0, 0, tiled=True)]
where the time goes in v3:
time: 138 us; the launch traced here: 137 us
  blocking collectives  47.3 us (34%)
  starting transfers between devices  42 us (30%)
  waiting for transfers between devices  29.7 us (22%)
  Pallas kernels  14 us (10%)
  local copies, waits for them, and re-layouts  3.26 us (2%)
    all_to_all x2, blocking collectives, exchanged(): return lax.all_to_all(value, axes, 0, 0, tiled=True)  47.3 us
    all_to_all x4, starting transfers between devices, exchanged(): return lax.all_to_all(value, axes, 0, 0, tiled=True)  22.5 us
    all_to_all x4, waiting for transfers between devices, exchanged(): return lax.all_to_all(value, axes, 0, 0, tiled=True)  22.1 us
    pallas_call x8, Pallas kernels, run(): return pl.pallas_call(kernel, **given)(*args)  14 us
    ppermute x1, starting transfers between devices, stencil(): z_next = lax.ppermute(low, GRP, back(n_grp))  5.75 us
    ppermute x1, waiting for transfers between devices, stencil(): x_prev = lax.ppermute(x_last, ROW, chain(n_row))  4.53 us
    ppermute x1, starting transfers between devices, stencil(): y_next = lax.ppermute(y_first, 'x', back(n_col))  4.41 us
    ppermute x1, starting transfers between devices, stencil(): x_prev = lax.ppermute(x_last, ROW, chain(n_row))  3.37 us
  transfers between devices with their start and end apart: 10, of which 4 were waited for; matrix products, arithmetic and copies ran while one was open for 1% of the time, Pallas kernels for 7%

profile of v3, /device:TPU:42, one launch (start us, length us, event | category | flops | bytes accessed | tf_op | source)
XLA Modules:
  0.0 137.0 jit_solution(14059862568836528821)
XLA Ops:
  0.6 0.0 copy-start
  0.6 5.2 %all-to-all-start = ((bf16[4,2,128,384]{3,2,1,0:T(8,128)(2,1)}), bf16[4,2,128,384]{3,2,1,0:T(8,128)(2,1)S(1)}, u32[]{:S(2)}, u32[]{:S(2)}) async-start(bf16[4,2,128,384]{3,2,1,0:T(8,128)(2,1)} %bitcast.25), calls=%async_computation | async-start | bytes 1572864 | tf_op jit(solution)/shard_map/all_to_all | solution.py:39
  5.9 10.2 %all-to-all-done.lines = bf16[4,2,128,384]{3,2,1,0:T(8,128)(2,1)S(1)} async-done(((bf16[4,2,128,384]{3,2,1,0:T(8,128)(2,1)}), bf16[4,2,128,384]{3,2,1,0:T(8,128)(2,1)S(1)}, u32[]{:S(2)}, u32[]{:S(2)}) %all-to-all-start) | async-done | bytes 786464 | tf_op jit(solution)/shard_map/all_to_all | solution.py:39
  16.2 1.2 shard_map.104
  17.3 32.5 %all_to_all.30.parts = f32[6,128,128]{2,1,0:T(8,128)S(1)} all-to-all(f32[6,128,128]{2,1,0:T(8,128)} %bitcast.23), channel_id=1, replica_groups=mesh['yh'=4,'core'=2,'yl'=2,'zh'=6,'zl'=2,'x'=4] {'zh'}, dimensions={0} | all-to-all | bytes 786432 | tf_op jit(solution)/shard_map/all_to_all | solution.py:39
  49.8 0.7 shard_map.105
  50.5 4.4 %all-to-all-start.2 = ((bf16[6,128,128]{2,1,0:T(8,128)(2,1)}), bf16[6,128,128]{2,1,0:T(8,128)(2,1)S(1)}, u32[]{:S(2)}, u32[]{:S(2)}) async-start(bf16[6,128,128]{2,1,0:T(8,128)(2,1)} %shard_map.105), calls=%async_computation.2 | async-start | bytes 393216 | tf_op jit(solution)/shard_map/all_to_all | solution.py:39
  54.9 0.9 constant_dynamic-slice_fusion.basis
  55.8 11.8 %all-to-all-done.2 = bf16[6,128,128]{2,1,0:T(8,128)(2,1)S(1)} async-done(((bf16[6,128,128]{2,1,0:T(8,128)(2,1)}), bf16[6,128,128]{2,1,0:T(8,128)(2,1)S(1)}, u32[]{:S(2)}, u32[]{:S(2)}) %all-to-all-start.2) | async-done | bytes 196640 | tf_op jit(solution)/shard_map/all_to_all | solution.py:39
  67.6 0.5 shard_map.106
  68.0 14.8 %all_to_all.31.parts = bf16[4,1024,128]{2,1,0:T(8,128)(2,1)S(1)} all-to-all(bf16[4,1024,128]{2,1,0:T(8,128)(2,1)S(1)} %shard_map.106), channel_id=1, replica_groups=mesh['yh'=4,'core'=2,'yl'=2,'zh'=6,'zl'=2,'x'=4] {'x'}, dimensions={0} | all-to-all | bytes 2097152 | tf_op jit(solution)/shard_map/all_to_all | solution.py:39
  82.9 0.9 shard_map.107
  83.8 5.7 %all-to-all-start.4 = ((bf16[4,400,128]{2,1,0:T(8,128)(2,1)}), bf16[4,400,128]{2,1,0:T(8,128)(2,1)S(1)}, u32[]{:S(2)}, u32[]{:S(2)}) async-start(bf16[4,400,128]{2,1,0:T(8,128)(2,1)} %shard_map.107), calls=%async_computation.4 | async-start | bytes 819200 | tf_op jit(solution)/shard_map/all_to_all | solution.py:39
  89.5 2.8 %shard_map.102 = (bf16[8,128,384]{2,1,0:T(8,128)(2,1)}, f32[8,1,384]{2,1,0:T(1,128)}, f32[8,1,384]{2,1,0:T(1,128)}, bf16[8,128,128]{2,1,0:T(8,128)(2,1)}, bf16[8,128,128]{2,1,0:T(8,128)(2,1)}) custom-call(f32[8,128,384]{2,1,0:T(8,128)S(1)} %bitcast.17), custom_call_target="tpu_custom_call" | custom-call | flops 100000000 | bytes 1048576 | tf_op jit(solution)/shard_map/pallas_call | solution.py:25
  92.3 1.9 %collective-permute-start = (bf16[8,128,384]{2,1,0:T(8,128)(2,1)}, bf16[8,128,384]{2,1,0:T(8,128)(2,1)S(1)}, u32[]{:S(2)}, u32[]{:S(2)}) collective-permute-start(bf16[8,128,384]{2,1,0:T(8,128)(2,1)} %get-tuple-element.13), channel_id=1, source_target_pairs={{0,96},{96,192},{192,288},{288,384},{384,480},{480,576},{576,672},... | collective-permute-start | bytes 2359304 | tf_op jit(solution)/shard_map/ppermute | solution.py:121
  94.2 5.8 %collective-permute-start.1 = (bf16[8,128,384]{2,1,0:T(8,128)(2,1)}, bf16[8,128,384]{2,1,0:T(8,128)(2,1)}, u32[]{:S(2)}, u32[]{:S(2)}) collective-permute-start(bf16[8,128,384]{2,1,0:T(8,128)(2,1)} %get-tuple-element.13), channel_id=1, source_target_pairs={{96,0},{192,96},{288,192},{384,288},{480,384},{576,480},{672,576},... | collective-permute-start | bytes 2359304 | tf_op jit(solution)/shard_map/ppermute | solution.py:122
  100.0 0.0 all-to-all-done.4.parts
  100.0 0.9 shard_map.108
  100.9 7.2 %all-to-all-start.5 = ((bf16[8,144,128]{2,1,0:T(8,128)(2,1)}), bf16[8,144,128]{2,1,0:T(8,128)(2,1)S(1)}, u32[]{:S(2)}, u32[]{:S(2)}) async-start(bf16[8,144,128]{2,1,0:T(8,128)(2,1)} %get-tuple-element.19), calls=%async_computation.5 | async-start | bytes 589824 | tf_op jit(solution)/shard_map/all_to_all | solution.py:39
  108.1 2.1 %collective-permute-start.4 = (bf16[8,128,128]{2,1,0:T(8,128)(2,1)}, bf16[8,128,128]{2,1,0:T(8,128)(2,1)}, u32[]{:S(2)}, u32[]{:S(2)}) collective-permute-start(bf16[8,128,128]{2,1,0:T(8,128)(2,1)} %get-tuple-element.16), channel_id=1, source_target_pairs={{0,1},{1,2},{2,3},{4,5},{5,6},{6,7},{8,9},{9,10},{10,11},{12,13},{... | collective-permute-start | bytes 786440 | tf_op jit(solution)/shard_map/ppermute | solution.py:125
  110.2 4.4 %collective-permute-start.5 = (bf16[8,128,128]{2,1,0:T(8,128)(2,1)}, bf16[8,128,128]{2,1,0:T(8,128)(2,1)}, u32[]{:S(2)}, u32[]{:S(2)}) collective-permute-start(bf16[8,128,128]{2,1,0:T(8,128)(2,1)} %get-tuple-element.17), channel_id=1, source_target_pairs={{1,0},{2,1},{3,2},{5,4},{6,5},{7,6},{9,8},{10,9},{11,10},{13,12},{... | collective-permute-start | bytes 786440 | tf_op jit(solution)/shard_map/ppermute | solution.py:126
  114.7 3.4 %collective-permute-start.2 = (f32[8,1,384]{2,1,0:T(1,128)}, f32[8,1,384]{2,1,0:T(1,128)S(1)}, u32[]{:S(2)}, u32[]{:S(2)}) collective-permute-start(f32[8,1,384]{2,1,0:T(1,128)} %get-tuple-element.14), channel_id=1, source_target_pairs={{0,4},{4,8},{8,12},{12,16},{16,20},{20,24},{24,28},{28,32},{32,36}... | collective-permute-start | bytes 36872 | tf_op jit(solution)/shard_map/ppermute | solution.py:123
  118.0 4.5 %collective-permute-done.2.xp = f32[8,1,384]{2,1,0:T(1,128)S(1)} collective-permute-done((f32[8,1,384]{2,1,0:T(1,128)}, f32[8,1,384]{2,1,0:T(1,128)S(1)}, u32[]{:S(2)}, u32[]{:S(2)}) %collective-permute-start.2) | collective-permute-done | bytes 12320 | tf_op jit(solution)/shard_map/ppermute | solution.py:123
  122.6 1.9 %collective-permute-start.3 = (f32[8,1,384]{2,1,0:T(1,128)}, f32[8,1,384]{2,1,0:T(1,128)S(1)}, u32[]{:S(2)}, u32[]{:S(2)}) collective-permute-start(f32[8,1,384]{2,1,0:T(1,128)} %get-tuple-element.15), channel_id=1, source_target_pairs={{4,0},{8,4},{12,8},{16,12},{20,16},{24,20},{28,24},{32,28},{36,32}... | collective-permute-start | bytes 36872 | tf_op jit(solution)/shard_map/ppermute | solution.py:124
  124.5 0.8 copy.11.speeds
  125.2 3.1 %collective-permute-done.3.xn = f32[8,1,384]{2,1,0:T(1,128)S(1)} collective-permute-done((f32[8,1,384]{2,1,0:T(1,128)}, f32[8,1,384]{2,1,0:T(1,128)S(1)}, u32[]{:S(2)}, u32[]{:S(2)}) %collective-permute-start.3) | collective-permute-done | bytes 12320 | tf_op jit(solution)/shard_map/ppermute | solution.py:124
  128.4 0.0 collective-permute-done.1.zn
  128.4 0.0 copy-start.2
  128.4 0.9 copy-done.2
  129.3 0.7 copy-done.3
  130.0 6.4 %shard_map.103 = f32[8,128,384]{2,1,0:T(8,128)} custom-call(f32[8]{0:T(128)S(1)} %copy-done.3, f32[8,3]{1,0:T(8,128)S(1)} %copy.11.speeds, f32[8,128,384]{2,1,0:T(8,128)S(1)} %bitcast.18, bf16[8,128,384]{2,1,0:T(8,128)(2,1)S(1)} %collective-permute-done.zp, bf16[8,128,384]{2,1,0:T(8,128)(2,1)} %collective-permute-done.1.zn, ...), custom_call_target="tpu_custom_call" | custom-call | flops 1000000000 | bytes 1048576 | tf_op jit(solution)/shard_map/pallas_call | solution.py:25
  136.3 0.7 shard_map.109
  (9 shorter events, 0.0 us)
Async XLA Ops:
  0.6 5.3 %copy-start = (bf16[3072,128]{1,0:T(8,128)(2,1)S(1)}, bf16[3072,128]{1,0:T(8,128)(2,1)}, u32[]{:S(2)}) copy-start(bf16[3072,128]{1,0:T(8,128)(2,1)} %param.12) | copy-start | bytes 2359300
  0.6 15.5 %all-to-all-start = ((bf16[4,2,128,384]{3,2,1,0:T(8,128)(2,1)}), bf16[4,2,128,384]{3,2,1,0:T(8,128)(2,1)S(1)}, u32[]{:S(2)}, u32[]{:S(2)}) async-start(bf16[4,2,128,384]{3,2,1,0:T(8,128)(2,1)} %bitcast.25), calls=%async_computation | async-start | bytes 1572864 | tf_op jit(solution)/shard_map/all_to_all | solution.py:39
  50.5 17.1 %all-to-all-start.2 = ((bf16[6,128,128]{2,1,0:T(8,128)(2,1)}), bf16[6,128,128]{2,1,0:T(8,128)(2,1)S(1)}, u32[]{:S(2)}, u32[]{:S(2)}) async-start(bf16[6,128,128]{2,1,0:T(8,128)(2,1)} %shard_map.105), calls=%async_computation.2 | async-start | bytes 393216 | tf_op jit(solution)/shard_map/all_to_all | solution.py:39
  82.9 6.6 %copy-start.1 = (f32[8,1,128,384]{3,2,1,0:T(8,128)S(1)}, f32[8,1,128,384]{3,2,1,0:T(8,128)}, u32[]{:S(2)}) copy-start(f32[8,1,128,384]{3,2,1,0:T(8,128)} %param.7) | copy-start | bytes 4718596
  83.8 16.1 %all-to-all-start.4 = ((bf16[4,400,128]{2,1,0:T(8,128)(2,1)}), bf16[4,400,128]{2,1,0:T(8,128)(2,1)S(1)}, u32[]{:S(2)}, u32[]{:S(2)}) async-start(bf16[4,400,128]{2,1,0:T(8,128)(2,1)} %shard_map.107), calls=%async_computation.4 | async-start | bytes 819200 | tf_op jit(solution)/shard_map/all_to_all | solution.py:39
  92.3 36.1 %collective-permute-start = (bf16[8,128,384]{2,1,0:T(8,128)(2,1)}, bf16[8,128,384]{2,1,0:T(8,128)(2,1)S(1)}, u32[]{:S(2)}, u32[]{:S(2)}) collective-permute-start(bf16[8,128,384]{2,1,0:T(8,128)(2,1)} %get-tuple-element.13), channel_id=1, source_target_pairs={{0,96},{96,192},{192,288},{288,384},{384,480},{480,576},{576,672},... | collective-permute-start | bytes 2359304 | tf_op jit(solution)/shard_map/ppermute | solution.py:121
  94.2 34.2 %collective-permute-start.1 = (bf16[8,128,384]{2,1,0:T(8,128)(2,1)}, bf16[8,128,384]{2,1,0:T(8,128)(2,1)}, u32[]{:S(2)}, u32[]{:S(2)}) collective-permute-start(bf16[8,128,384]{2,1,0:T(8,128)(2,1)} %get-tuple-element.13), channel_id=1, source_target_pairs={{96,0},{192,96},{288,192},{384,288},{480,384},{576,480},{672,576},... | collective-permute-start | bytes 2359304 | tf_op jit(solution)/shard_map/ppermute | solution.py:122
  100.9 35.4 %all-to-all-start.5 = ((bf16[8,144,128]{2,1,0:T(8,128)(2,1)}), bf16[8,144,128]{2,1,0:T(8,128)(2,1)S(1)}, u32[]{:S(2)}, u32[]{:S(2)}) async-start(bf16[8,144,128]{2,1,0:T(8,128)(2,1)} %get-tuple-element.19), calls=%async_computation.5 | async-start | bytes 589824 | tf_op jit(solution)/shard_map/all_to_all | solution.py:39
  108.1 20.2 %collective-permute-start.4 = (bf16[8,128,128]{2,1,0:T(8,128)(2,1)}, bf16[8,128,128]{2,1,0:T(8,128)(2,1)}, u32[]{:S(2)}, u32[]{:S(2)}) collective-permute-start(bf16[8,128,128]{2,1,0:T(8,128)(2,1)} %get-tuple-element.16), channel_id=1, source_target_pairs={{0,1},{1,2},{2,3},{4,5},{5,6},{6,7},{8,9},{9,10},{10,11},{12,13},{... | collective-permute-start | bytes 786440 | tf_op jit(solution)/shard_map/ppermute | solution.py:125
  110.2 18.1 %collective-permute-start.5 = (bf16[8,128,128]{2,1,0:T(8,128)(2,1)}, bf16[8,128,128]{2,1,0:T(8,128)(2,1)}, u32[]{:S(2)}, u32[]{:S(2)}) collective-permute-start(bf16[8,128,128]{2,1,0:T(8,128)(2,1)} %get-tuple-element.17), channel_id=1, source_target_pairs={{1,0},{2,1},{3,2},{5,4},{6,5},{7,6},{9,8},{10,9},{11,10},{13,12},{... | collective-permute-start | bytes 786440 | tf_op jit(solution)/shard_map/ppermute | solution.py:126
  114.7 7.9 %collective-permute-start.2 = (f32[8,1,384]{2,1,0:T(1,128)}, f32[8,1,384]{2,1,0:T(1,128)S(1)}, u32[]{:S(2)}, u32[]{:S(2)}) collective-permute-start(f32[8,1,384]{2,1,0:T(1,128)} %get-tuple-element.14), channel_id=1, source_target_pairs={{0,4},{4,8},{8,12},{12,16},{16,20},{20,24},{24,28},{28,32},{32,36}... | collective-permute-start | bytes 36872 | tf_op jit(solution)/shard_map/ppermute | solution.py:123
  122.6 5.8 %collective-permute-start.3 = (f32[8,1,384]{2,1,0:T(1,128)}, f32[8,1,384]{2,1,0:T(1,128)S(1)}, u32[]{:S(2)}, u32[]{:S(2)}) collective-permute-start(f32[8,1,384]{2,1,0:T(1,128)} %get-tuple-element.15), channel_id=1, source_target_pairs={{4,0},{8,4},{12,8},{16,12},{20,16},{24,20},{28,24},{32,28},{36,32}... | collective-permute-start | bytes 36872 | tf_op jit(solution)/shard_map/ppermute | solution.py:124
  128.4 0.9 copy-start.2
  129.3 0.7 copy-start.3

commit v4 on v3

--- a/solution.py
+++ b/solution.py
@@ -157,36 +157,34 @@
         out[k] = low
 
 
-def moments_kernel(scale, lines, projected, basis, out):
+def moments_kernel(scale, lines, projected, basis, out, rest):
     quad, own, wx, wy = lines.shape
     rank = projected.shape[-1]
     columns = out.shape[0]
     for s in range(own):
         core = dot_t(projected[s], basis[...])
         high = core.astype(BF16)
-        low = (core - high.astype(F32)).astype(BF16)
+        rest[pl.ds(s * rank, rank)] = core - high.astype(F32)
         for k in range(columns):
             out[k, pl.ds(s * rank, rank)] = high
-            out[k, pl.ds((own + s) * rank, rank)] = low
     total = dot(lines[:, 0].reshape(quad * wx, wy), projected[0])
     for s in range(1, own):
         total = total + dot(lines[:, s].reshape(quad * wx, wy), projected[s])
     total = (scale * total).astype(BF16)
     for k in range(columns):
-        out[k, pl.ds(2 * own * rank, quad * wx)] = total
-
-
-def mix_kernel(scale, zh, parts, projected, out):
+        out[k, pl.ds(own * rank, quad * wx)] = total
+
+
+def mix_kernel(scale, zh, parts, rest, projected, out):
     own, wy, rank = projected.shape
     columns, quad = parts.shape[0], out.shape[0]
-    part = (parts.shape[1] - 2 * own * rank) // quad
+    part = (parts.shape[1] - own * rank) // quad
     half_rows = 2 * (out.shape[1] - own * rank - part)
     totals = [0.0, 0.0]
     for s in range(own):
-        total = 0.0
-        for first in (s * rank, (own + s) * rank):
-            for k in range(columns):
-                total = total + parts[k, pl.ds(first, rank)].astype(F32)
+        total = rest[pl.ds(s * rank, rank)]
+        for k in range(columns):
+            total = total + parts[k, pl.ds(s * rank, rank)].astype(F32)
         low = total.astype(BF16)
         for q in range(quad):
             out[q, pl.ds(s * rank, rank)] = low
@@ -196,7 +194,7 @@
     for q in range(quad):
         total = 0.0
         for k in range(columns):
-            total = total + parts[k, pl.ds(2 * own * rank + q * part, part)].astype(F32)
+            total = total + parts[k, pl.ds(own * rank + q * part, part)].astype(F32)
         out[q, pl.ds(own * rank, part)] = total.astype(BF16)
     for h in range(2):
         rows = (scale * totals[h]).astype(BF16)
@@ -263,22 +261,25 @@
     )(arrived)
     projected = exchanged(mine, "zh").reshape(own, width_y, rank)
 
-    moments = call(
+    moments, rest = call(
         functools.partial(moments_kernel, scale_x),
         in_specs=[WHOLE, WHOLE, WHOLE],
-        out_specs=WHOLE,
-        out_shape=shape((n_col, 2 * own * rank + n_quad * width_x, rank), BF16),
+        out_specs=[WHOLE, WHOLE],
+        out_shape=[
+            shape((n_col, own * rank + n_quad * width_x, rank), BF16),
+            shape((own * rank, rank), F32),
+        ],
         cost_estimate=cost(4 * n_quad * width_x * own * width_y * rank),
         compiler_params=GRANT,
     )(lines, projected, by)
     mixed = call(
         functools.partial(mix_kernel, scale_y),
-        in_specs=[SCALARS, WHOLE, WHOLE],
+        in_specs=[SCALARS, WHOLE, WHOLE, WHOLE],
         out_specs=WHOLE,
         out_shape=shape((n_quad, own * rank + width_x + part_y, rank), BF16),
         cost_estimate=cost(10**8),
         compiler_params=GRANT,
-    )(zh.reshape(1), exchanged(moments, "x"), projected)
+    )(zh.reshape(1), exchanged(moments, "x"), rest, projected)
     core, rows = call(
         spread_kernel,
         in_specs=[WHOLE],

time: 138 us -> 136 us (0.986)
  blocking collectives: 47.3 us -> 45.3 us
    all_to_all x2, blocking collectives: 47.3 us -> 45.3 us  [exchanged(): return lax.all_to_all(value, axes, 0, 0, tiled=True)]
where the time goes in v4:
time: 136 us; the launch traced here: 135 us
  blocking collectives  45.3 us (33%)
  starting transfers between devices  41.6 us (31%)
  waiting for transfers between devices  29.7 us (22%)
  Pallas kernels  13.9 us (10%)
  local copies, waits for them, and re-layouts  3.26 us (2%)
    all_to_all x2, blocking collectives, exchanged(): return lax.all_to_all(value, axes, 0, 0, tiled=True)  45.3 us
    all_to_all x4, starting transfers between devices, exchanged(): return lax.all_to_all(value, axes, 0, 0, tiled=True)  22.1 us
    all_to_all x4, waiting for transfers between devices, exchanged(): return lax.all_to_all(value, axes, 0, 0, tiled=True)  22.1 us
    pallas_call x8, Pallas kernels, run(): return pl.pallas_call(kernel, **given)(*args)  13.9 us
    ppermute x1, starting transfers between devices, stencil(): z_next = lax.ppermute(low, GRP, back(n_grp))  5.75 us
    ppermute x1, waiting for transfers between devices, stencil(): x_prev = lax.ppermute(x_last, ROW, chain(n_row))  4.53 us
    ppermute x1, starting transfers between devices, stencil(): y_next = lax.ppermute(y_first, 'x', back(n_col))  4.41 us
    ppermute x1, starting transfers between devices, stencil(): x_prev = lax.ppermute(x_last, ROW, chain(n_row))  3.37 us
  transfers between devices with their start and end apart: 10, of which 4 were waited for; matrix products, arithmetic and copies ran while one was open for 1% of the time, Pallas kernels for 7%

profile of v4, /device:TPU:42, one launch (start us, length us, event | category | flops | bytes accessed | tf_op | source)
XLA Modules:
  0.0 134.5 jit_solution(8715171400612593902)
XLA Ops:
  0.6 0.0 copy-start
  0.6 5.2 %all-to-all-start = ((bf16[4,2,128,384]{3,2,1,0:T(8,128)(2,1)}), bf16[4,2,128,384]{3,2,1,0:T(8,128)(2,1)S(1)}, u32[]{:S(2)}, u32[]{:S(2)}) async-start(bf16[4,2,128,384]{3,2,1,0:T(8,128)(2,1)} %bitcast.25), calls=%async_computation | async-start | bytes 1572864 | tf_op jit(solution)/shard_map/all_to_all | solution.py:39
  5.9 10.2 %all-to-all-done.lines = bf16[4,2,128,384]{3,2,1,0:T(8,128)(2,1)S(1)} async-done(((bf16[4,2,128,384]{3,2,1,0:T(8,128)(2,1)}), bf16[4,2,128,384]{3,2,1,0:T(8,128)(2,1)S(1)}, u32[]{:S(2)}, u32[]{:S(2)}) %all-to-all-start) | async-done | bytes 786464 | tf_op jit(solution)/shard_map/all_to_all | solution.py:39
  16.2 1.2 shard_map.104
  17.3 32.5 %all_to_all.30.parts = f32[6,128,128]{2,1,0:T(8,128)S(1)} all-to-all(f32[6,128,128]{2,1,0:T(8,128)} %bitcast.23), channel_id=1, replica_groups=mesh['yh'=4,'core'=2,'yl'=2,'zh'=6,'zl'=2,'x'=4] {'zh'}, dimensions={0} | all-to-all | bytes 786432 | tf_op jit(solution)/shard_map/all_to_all | solution.py:39
  49.8 0.7 shard_map.105
  50.5 4.4 %all-to-all-start.2 = ((bf16[6,128,128]{2,1,0:T(8,128)(2,1)}), bf16[6,128,128]{2,1,0:T(8,128)(2,1)S(1)}, u32[]{:S(2)}, u32[]{:S(2)}) async-start(bf16[6,128,128]{2,1,0:T(8,128)(2,1)} %shard_map.105), calls=%async_computation.2 | async-start | bytes 393216 | tf_op jit(solution)/shard_map/all_to_all | solution.py:39
  54.9 0.9 constant_dynamic-slice_fusion.basis
  55.8 11.8 %all-to-all-done.2 = bf16[6,128,128]{2,1,0:T(8,128)(2,1)S(1)} async-done(((bf16[6,128,128]{2,1,0:T(8,128)(2,1)}), bf16[6,128,128]{2,1,0:T(8,128)(2,1)S(1)}, u32[]{:S(2)}, u32[]{:S(2)}) %all-to-all-start.2) | async-done | bytes 196640 | tf_op jit(solution)/shard_map/all_to_all | solution.py:39
  67.6 0.5 shard_map.106
  68.0 0.0 copy-start.1
  68.1 12.8 %all_to_all.31.parts = bf16[4,768,128]{2,1,0:T(8,128)(2,1)S(1)} all-to-all(bf16[4,768,128]{2,1,0:T(8,128)(2,1)S(1)} %get-tuple-element.20), channel_id=1, replica_groups=mesh['yh'=4,'core'=2,'yl'=2,'zh'=6,'zl'=2,'x'=4] {'x'}, dimensions={0} | all-to-all | bytes 1572864 | tf_op jit(solution)/shard_map/all_to_all | solution.py:39
  80.8 0.9 shard_map.107
  81.8 5.3 %all-to-all-start.4 = ((bf16[4,400,128]{2,1,0:T(8,128)(2,1)}), bf16[4,400,128]{2,1,0:T(8,128)(2,1)S(1)}, u32[]{:S(2)}, u32[]{:S(2)}) async-start(bf16[4,400,128]{2,1,0:T(8,128)(2,1)} %shard_map.107), calls=%async_computation.4 | async-start | bytes 819200 | tf_op jit(solution)/shard_map/all_to_all | solution.py:39
  87.1 2.8 %shard_map.102 = (bf16[8,128,384]{2,1,0:T(8,128)(2,1)}, f32[8,1,384]{2,1,0:T(1,128)}, f32[8,1,384]{2,1,0:T(1,128)}, bf16[8,128,128]{2,1,0:T(8,128)(2,1)}, bf16[8,128,128]{2,1,0:T(8,128)(2,1)}) custom-call(f32[8,128,384]{2,1,0:T(8,128)S(1)} %bitcast.17), custom_call_target="tpu_custom_call" | custom-call | flops 100000000 | bytes 1048576 | tf_op jit(solution)/shard_map/pallas_call | solution.py:25
  89.8 1.9 %collective-permute-start = (bf16[8,128,384]{2,1,0:T(8,128)(2,1)}, bf16[8,128,384]{2,1,0:T(8,128)(2,1)S(1)}, u32[]{:S(2)}, u32[]{:S(2)}) collective-permute-start(bf16[8,128,384]{2,1,0:T(8,128)(2,1)} %get-tuple-element.15), channel_id=1, source_target_pairs={{0,96},{96,192},{192,288},{288,384},{384,480},{480,576},{576,672},... | collective-permute-start | bytes 2359304 | tf_op jit(solution)/shard_map/ppermute | solution.py:121
  91.7 5.8 %collective-permute-start.1 = (bf16[8,128,384]{2,1,0:T(8,128)(2,1)}, bf16[8,128,384]{2,1,0:T(8,128)(2,1)}, u32[]{:S(2)}, u32[]{:S(2)}) collective-permute-start(bf16[8,128,384]{2,1,0:T(8,128)(2,1)} %get-tuple-element.15), channel_id=1, source_target_pairs={{96,0},{192,96},{288,192},{384,288},{480,384},{576,480},{672,576},... | collective-permute-start | bytes 2359304 | tf_op jit(solution)/shard_map/ppermute | solution.py:122
  97.5 0.9 shard_map.108
  98.4 7.2 %all-to-all-start.5 = ((bf16[8,144,128]{2,1,0:T(8,128)(2,1)}), bf16[8,144,128]{2,1,0:T(8,128)(2,1)S(1)}, u32[]{:S(2)}, u32[]{:S(2)}) async-start(bf16[8,144,128]{2,1,0:T(8,128)(2,1)} %get-tuple-element.23), calls=%async_computation.5 | async-start | bytes 589824 | tf_op jit(solution)/shard_map/all_to_all | solution.py:39
  105.6 2.1 %collective-permute-start.4 = (bf16[8,128,128]{2,1,0:T(8,128)(2,1)}, bf16[8,128,128]{2,1,0:T(8,128)(2,1)}, u32[]{:S(2)}, u32[]{:S(2)}) collective-permute-start(bf16[8,128,128]{2,1,0:T(8,128)(2,1)} %get-tuple-element.18), channel_id=1, source_target_pairs={{0,1},{1,2},{2,3},{4,5},{5,6},{6,7},{8,9},{9,10},{10,11},{12,13},{... | collective-permute-start | bytes 786440 | tf_op jit(solution)/shard_map/ppermute | solution.py:125
  107.7 4.4 %collective-permute-start.5 = (bf16[8,128,128]{2,1,0:T(8,128)(2,1)}, bf16[8,128,128]{2,1,0:T(8,128)(2,1)}, u32[]{:S(2)}, u32[]{:S(2)}) collective-permute-start(bf16[8,128,128]{2,1,0:T(8,128)(2,1)} %get-tuple-element.19), channel_id=1, source_target_pairs={{1,0},{2,1},{3,2},{5,4},{6,5},{7,6},{9,8},{10,9},{11,10},{13,12},{... | collective-permute-start | bytes 786440 | tf_op jit(solution)/shard_map/ppermute | solution.py:126
  112.2 3.4 %collective-permute-start.2 = (f32[8,1,384]{2,1,0:T(1,128)}, f32[8,1,384]{2,1,0:T(1,128)S(1)}, u32[]{:S(2)}, u32[]{:S(2)}) collective-permute-start(f32[8,1,384]{2,1,0:T(1,128)} %get-tuple-element.16), channel_id=1, source_target_pairs={{0,4},{4,8},{8,12},{12,16},{16,20},{20,24},{24,28},{28,32},{32,36}... | collective-permute-start | bytes 36872 | tf_op jit(solution)/shard_map/ppermute | solution.py:123
  115.5 4.5 %collective-permute-done.2.xp = f32[8,1,384]{2,1,0:T(1,128)S(1)} collective-permute-done((f32[8,1,384]{2,1,0:T(1,128)}, f32[8,1,384]{2,1,0:T(1,128)S(1)}, u32[]{:S(2)}, u32[]{:S(2)}) %collective-permute-start.2) | collective-permute-done | bytes 12320 | tf_op jit(solution)/shard_map/ppermute | solution.py:123
  120.1 1.9 %collective-permute-start.3 = (f32[8,1,384]{2,1,0:T(1,128)}, f32[8,1,384]{2,1,0:T(1,128)S(1)}, u32[]{:S(2)}, u32[]{:S(2)}) collective-permute-start(f32[8,1,384]{2,1,0:T(1,128)} %get-tuple-element.17), channel_id=1, source_target_pairs={{4,0},{8,4},{12,8},{16,12},{20,16},{24,20},{28,24},{32,28},{36,32}... | collective-permute-start | bytes 36872 | tf_op jit(solution)/shard_map/ppermute | solution.py:124
  122.0 0.8 copy.11.speeds
  122.7 3.1 %collective-permute-done.3.xn = f32[8,1,384]{2,1,0:T(1,128)S(1)} collective-permute-done((f32[8,1,384]{2,1,0:T(1,128)}, f32[8,1,384]{2,1,0:T(1,128)S(1)}, u32[]{:S(2)}, u32[]{:S(2)}) %collective-permute-start.3) | collective-permute-done | bytes 12320 | tf_op jit(solution)/shard_map/ppermute | solution.py:124
  125.9 0.0 collective-permute-done.1.zn
  125.9 0.0 copy-start.2
  125.9 0.9 copy-done.2
  126.8 0.7 copy-done.3
  127.5 6.4 %shard_map.103 = f32[8,128,384]{2,1,0:T(8,128)} custom-call(f32[8]{0:T(128)S(1)} %copy-done.3, f32[8,3]{1,0:T(8,128)S(1)} %copy.11.speeds, f32[8,128,384]{2,1,0:T(8,128)S(1)} %bitcast.18, bf16[8,128,384]{2,1,0:T(8,128)(2,1)S(1)} %collective-permute-done.zp, bf16[8,128,384]{2,1,0:T(8,128)(2,1)} %collective-permute-done.1.zn, ...), custom_call_target="tpu_custom_call" | custom-call | flops 1000000000 | bytes 1048576 | tf_op jit(solution)/shard_map/pallas_call | solution.py:25
  133.8 0.7 shard_map.109
  (9 shorter events, 0.0 us)
Async XLA Ops:
  0.6 5.3 %copy-start = (bf16[3072,128]{1,0:T(8,128)(2,1)S(1)}, bf16[3072,128]{1,0:T(8,128)(2,1)}, u32[]{:S(2)}) copy-start(bf16[3072,128]{1,0:T(8,128)(2,1)} %param.12) | copy-start | bytes 2359300
  0.6 15.5 %all-to-all-start = ((bf16[4,2,128,384]{3,2,1,0:T(8,128)(2,1)}), bf16[4,2,128,384]{3,2,1,0:T(8,128)(2,1)S(1)}, u32[]{:S(2)}, u32[]{:S(2)}) async-start(bf16[4,2,128,384]{3,2,1,0:T(8,128)(2,1)} %bitcast.25), calls=%async_computation | async-start | bytes 1572864 | tf_op jit(solution)/shard_map/all_to_all | solution.py:39
  50.5 17.1 %all-to-all-start.2 = ((bf16[6,128,128]{2,1,0:T(8,128)(2,1)}), bf16[6,128,128]{2,1,0:T(8,128)(2,1)S(1)}, u32[]{:S(2)}, u32[]{:S(2)}) async-start(bf16[6,128,128]{2,1,0:T(8,128)(2,1)} %shard_map.105), calls=%async_computation.2 | async-start | bytes 393216 | tf_op jit(solution)/shard_map/all_to_all | solution.py:39
  68.0 19.0 %copy-start.1 = (f32[8,1,128,384]{3,2,1,0:T(8,128)S(1)}, f32[8,1,128,384]{3,2,1,0:T(8,128)}, u32[]{:S(2)}) copy-start(f32[8,1,128,384]{3,2,1,0:T(8,128)} %param.7) | copy-start | bytes 4718596
  81.8 15.7 %all-to-all-start.4 = ((bf16[4,400,128]{2,1,0:T(8,128)(2,1)}), bf16[4,400,128]{2,1,0:T(8,128)(2,1)S(1)}, u32[]{:S(2)}, u32[]{:S(2)}) async-start(bf16[4,400,128]{2,1,0:T(8,128)(2,1)} %shard_map.107), calls=%async_computation.4 | async-start | bytes 819200 | tf_op jit(solution)/shard_map/all_to_all | solution.py:39
  89.8 36.1 %collective-permute-start = (bf16[8,128,384]{2,1,0:T(8,128)(2,1)}, bf16[8,128,384]{2,1,0:T(8,128)(2,1)S(1)}, u32[]{:S(2)}, u32[]{:S(2)}) collective-permute-start(bf16[8,128,384]{2,1,0:T(8,128)(2,1)} %get-tuple-element.15), channel_id=1, source_target_pairs={{0,96},{96,192},{192,288},{288,384},{384,480},{480,576},{576,672},... | collective-permute-start | bytes 2359304 | tf_op jit(solution)/shard_map/ppermute | solution.py:121
  91.7 34.1 %collective-permute-start.1 = (bf16[8,128,384]{2,1,0:T(8,128)(2,1)}, bf16[8,128,384]{2,1,0:T(8,128)(2,1)}, u32[]{:S(2)}, u32[]{:S(2)}) collective-permute-start(bf16[8,128,384]{2,1,0:T(8,128)(2,1)} %get-tuple-element.15), channel_id=1, source_target_pairs={{96,0},{192,96},{288,192},{384,288},{480,384},{576,480},{672,576},... | collective-permute-start | bytes 2359304 | tf_op jit(solution)/shard_map/ppermute | solution.py:122
  98.4 35.4 %all-to-all-start.5 = ((bf16[8,144,128]{2,1,0:T(8,128)(2,1)}), bf16[8,144,128]{2,1,0:T(8,128)(2,1)S(1)}, u32[]{:S(2)}, u32[]{:S(2)}) async-start(bf16[8,144,128]{2,1,0:T(8,128)(2,1)} %get-tuple-element.23), calls=%async_computation.5 | async-start | bytes 589824 | tf_op jit(solution)/shard_map/all_to_all | solution.py:39
  105.6 20.2 %collective-permute-start.4 = (bf16[8,128,128]{2,1,0:T(8,128)(2,1)}, bf16[8,128,128]{2,1,0:T(8,128)(2,1)}, u32[]{:S(2)}, u32[]{:S(2)}) collective-permute-start(bf16[8,128,128]{2,1,0:T(8,128)(2,1)} %get-tuple-element.18), channel_id=1, source_target_pairs={{0,1},{1,2},{2,3},{4,5},{5,6},{6,7},{8,9},{9,10},{10,11},{12,13},{... | collective-permute-start | bytes 786440 | tf_op jit(solution)/shard_map/ppermute | solution.py:125
  107.7 18.1 %collective-permute-start.5 = (bf16[8,128,128]{2,1,0:T(8,128)(2,1)}, bf16[8,128,128]{2,1,0:T(8,128)(2,1)}, u32[]{:S(2)}, u32[]{:S(2)}) collective-permute-start(bf16[8,128,128]{2,1,0:T(8,128)(2,1)} %get-tuple-element.19), channel_id=1, source_target_pairs={{1,0},{2,1},{3,2},{5,4},{6,5},{7,6},{9,8},{10,9},{11,10},{13,12},{... | collective-permute-start | bytes 786440 | tf_op jit(solution)/shard_map/ppermute | solution.py:126
  112.2 7.9 %collective-permute-start.2 = (f32[8,1,384]{2,1,0:T(1,128)}, f32[8,1,384]{2,1,0:T(1,128)S(1)}, u32[]{:S(2)}, u32[]{:S(2)}) collective-permute-start(f32[8,1,384]{2,1,0:T(1,128)} %get-tuple-element.16), channel_id=1, source_target_pairs={{0,4},{4,8},{8,12},{12,16},{16,20},{20,24},{24,28},{28,32},{32,36}... | collective-permute-start | bytes 36872 | tf_op jit(solution)/shard_map/ppermute | solution.py:123
  120.1 5.8 %collective-permute-start.3 = (f32[8,1,384]{2,1,0:T(1,128)}, f32[8,1,384]{2,1,0:T(1,128)S(1)}, u32[]{:S(2)}, u32[]{:S(2)}) collective-permute-start(f32[8,1,384]{2,1,0:T(1,128)} %get-tuple-element.17), channel_id=1, source_target_pairs={{4,0},{8,4},{12,8},{16,12},{20,16},{24,20},{28,24},{32,28},{36,32}... | collective-permute-start | bytes 36872 | tf_op jit(solution)/shard_map/ppermute | solution.py:124
  125.9 0.9 copy-start.2
  126.8 0.7 copy-start.3
